TPU v7x, 256 devices: a whole 4x4x8 slice. The times are simulated.
256 devices in a mesh: rp: 64 (over y, x, z_hi, core), re: 4 (over z_lo).
Axes of the slice: x: 4, y: 4, z: 8 (z_hi: 2, z_lo: 4; z = z_hi * 4 + z_lo), core: 2. Of those that a mesh axis runs over, the one named last changes fastest.
Arguments:
- coupling: bfloat16 [1024, 4, 2, 6, 4096], P('rp', 're'), may hold values from -0.4375 to 0.4375
- rp_coords: int32 [3, 1024], P(None, 'rp'), may hold values from -8 to 8
- degeneracy: int32 [1024], P('rp'), may hold values from 1 to 8
- qpoints: int32 [3, 512], replicated, may hold values from 0 to 15
- eigvec: float32 [512, 2, 6, 6], P('rp'), may hold values from -1.75 to 1.75
Outputs:
- coupling_q: float32 [512, 4, 2, 6, 4096], P('rp', None, None, None, 're')
All inputs are finite; a program needn't handle non-finite values.
Results may differ from a plain program's by a relative error of at most 0.0042.
Values may be sent and summed in bfloat16 or wider, within the bound.
No kernel may reach another device: no remote copies, remote signals or barrier semaphores. Data moves between devices by JAX's collectives and lax.ppermute only.
A program may use at most 64 MiB of HBM per device.

v0:
```python
import math

import jax
import jax.numpy as jnp
from jax import lax
from jax.sharding import PartitionSpec as P

QGRID = 16


def laid_out(tiles, dim):
    dims = list(tiles.shape[1:])
    dims[dim] *= tiles.shape[0]
    return jnp.moveaxis(tiles, 0, dim).reshape(dims)


def from_everyone(x, axis):
    peers = lax.axis_size(axis)
    return lax.all_to_all(jnp.broadcast_to(x[None], (peers, *x.shape)), axis, 0, 0, tiled=True)


def gathered_copies(x, axis, dim):
    return laid_out(from_everyone(x, axis), dim)


def in_blocks(x, dim, peers):
    before, after = (x.shape[:dim], x.shape[dim + 1 :])
    return jnp.moveaxis(x.reshape(*before, peers, -1, *after), dim, 0)


def joined_exchange(x, axis, axes, splits, concats):
    sizes = [lax.axis_size(a) for a in axes]
    tiles = in_blocks(x, splits[0], sizes[0])
    tiles = jnp.moveaxis(in_blocks(tiles, splits[1] + 1, sizes[1]), 0, 1)
    inside = tiles.shape[2:]
    tiles = tiles.reshape(-1, *inside)
    tiles = lax.all_to_all(tiles, axis, split_axis=0, concat_axis=0, tiled=True)
    tiles = laid_out(tiles.reshape(*sizes, *inside), concats[0] + 1)
    return laid_out(tiles, concats[1])


def phases(points, coords, degeneracy):
    turns = jnp.mod(points[0][:, None] * coords[0][None, :], QGRID)
    turns = turns + jnp.mod(points[1][:, None] * coords[1][None, :], QGRID)
    turns = turns + jnp.mod(points[2][:, None] * coords[2][None, :], QGRID)
    turns = jnp.mod(turns, QGRID)
    angles = turns.astype(jnp.float32) * (2.0 * math.pi / QGRID)
    weights = 1.0 / degeneracy.astype(jnp.float32)
    table = jnp.concatenate(
        [jnp.cos(angles) * weights[None, :], jnp.sin(angles) * weights[None, :]], axis=0
    )
    return table.astype(jnp.bfloat16)


def combine(table, coupling):
    point_count = table.shape[0] // 2
    product = jnp.dot(
        table, coupling.reshape(coupling.shape[0], -1), preferred_element_type=jnp.float32
    )
    product = product.reshape((2, point_count) + coupling.shape[1:])
    real_part = product[0, :, :, 0] - product[1, :, :, 1]
    imag_part = product[0, :, :, 1] + product[1, :, :, 0]
    return jnp.stack([real_part, imag_part], axis=2)


def mode_mix(values, matrix):
    return jnp.einsum("qrkp,qkn->qrnp", values, matrix, precision=lax.Precision.HIGHEST)


def rotate(summed, eigvec):
    real_in = summed[:, :, 0]
    imag_in = summed[:, :, 1]
    vec_real = eigvec[:, 0]
    vec_imag = eigvec[:, 1]
    real_out = mode_mix(real_in, vec_real) - mode_mix(imag_in, vec_imag)
    imag_out = mode_mix(real_in, vec_imag) + mode_mix(imag_in, vec_real)
    return jnp.stack([real_out, imag_out], axis=2)


def to_owners(all_points):
    return lax.all_to_all(
        all_points.astype(jnp.bfloat16), "rp", split_axis=0, concat_axis=3, tiled=True
    ).astype(all_points.dtype)


def per_device(coupling, rp_coords, degeneracy, qpoints, eigvec):
    stacked = jnp.concatenate([rp_coords, degeneracy[None, :]], axis=0)
    lattice = gathered_copies(stacked, "rp", 1)
    table = phases(qpoints, lattice[:3], lattice[3])
    rp_count = lax.axis_size("rp")
    re_count = lax.axis_size("re")
    local_rp, local_re, parts, mode_count, pair_count = coupling.shape
    q_local = eigvec.shape[0]
    pair_share = pair_count // re_count
    block_cols = mode_count * pair_share
    inner = block_cols // rp_count
    reordered = coupling.reshape(local_rp, local_re, parts, mode_count, re_count, pair_share)
    reordered = jnp.swapaxes(reordered, 3, 4)
    reordered = reordered.reshape(local_rp, local_re, parts, re_count, rp_count, inner)
    reordered = jnp.swapaxes(reordered, 3, 4)
    reordered = reordered.reshape(local_rp, local_re, parts, rp_count * re_count * inner)
    moved = joined_exchange(reordered, ("rp", "re"), ("rp", "re"), (3, 3), (0, 1))
    all_points = combine(table, moved)
    summed = to_owners(all_points)
    summed = summed.reshape(q_local, summed.shape[1], parts, mode_count, pair_share)
    return rotate(summed, eigvec)


def solution(mesh):
    return jax.shard_map(
        per_device,
        mesh=mesh,
        in_specs=(
            P("rp", "re", None, None, None),
            P(None, "rp"),
            P("rp"),
            P(),
            P("rp", None, None, None),
        ),
        out_specs=P("rp", None, None, None, "re"),
        check_vma=False,
    )
```

profile of v0, /device:TPU:33, one launch (start us, length us, event | category | flops | bytes accessed | tf_op | source)
XLA Modules:
  0.0 161.4 jit_solution(17689326410087397459)
XLA Ops:
  0.0 0.7 pad_add_fusion
  0.7 0.7 broadcast_in_dim.5
  1.4 13.9 %all-to-all-start = ((s32[64,4,16]{2,1,0:T(4,128)}), s32[64,4,16]{2,1,0:T(4,128)S(1)}, u32[]{:S(2)}, u32[]{:S(2)}) async-start(s32[64,4,16]{2,1,0:T(4,128)} %broadcast_in_dim.5), calls=%async_computation | async-start | bytes 262144 | tf_op jit(solution)/shard_map/all_to_all | solution.py:19
  15.3 3.7 %reshape.92 = bf16[16,1,2,6,4,1024]{5,4,2,3,0,1:T(4,128)(2,1)} reshape(bf16[16,1,2,6,4096]{4,2,3,1,0:T(2,128)(2,1)} %param.5) | data formatting | bytes 3145728 | tf_op jit(solution)/shard_map/reshape | solution.py:97
  19.0 2.5 %copy.68 = bf16[16,1,2,6,4,1024]{5,3,4,2,0,1:T(8,128)(2,1)S(1)} copy(bf16[16,1,2,6,4,1024]{5,4,2,3,0,1:T(4,128)(2,1)} %reshape.92) | data formatting | bytes 3145728 | tf_op jit(solution)/shard_map/reshape | solution.py:97
  21.5 3.5 %reshape.93 = bf16[16,1,2,4,64,96]{5,4,3,2,0,1:T(8,128)(2,1)} reshape(bf16[16,1,2,4,6,1024]{5,4,3,2,0,1:T(8,128)(2,1)S(1)} %bitcast.98) | data formatting | bytes 3145728 | tf_op jit(solution)/shard_map/reshape | solution.py:99
  25.0 4.9 %copy.42 = bf16[16,1,2,64,4,96]{5,4,3,2,0,1:T(4,128)(2,1)} copy(bf16[16,1,2,64,4,96]{5,3,4,2,0,1:T(8,128)(2,1)} %bitcast.101) | data formatting | bytes 3145728 | tf_op jit(solution)/shard_map/transpose | solution.py:100
  29.8 3.5 %reshape_reshape.6 = bf16[16,1,2,64,384]{4,3,2,0,1:T(8,128)(2,1)S(1)} reshape(bf16[16,1,2,64,4,96]{5,4,3,2,0,1:T(4,128)(2,1)} %copy.42) | data formatting | bytes 3145728 | tf_op jit(solution)/shard_map/reshape;reshape | solution.py:28
  33.3 0.6 fusion.25
  33.9 0.5 pad_maximum_fusion.1
  34.4 1.4 copy.43
  35.8 1.7 %copy.44 = bf16[256,16,1,2,96]{4,1,3,2,0:T(8,128)(2,1)} copy(bf16[256,16,1,2,96]{4,1,0,3,2:T(8,128)(2,1)S(1)} %bitcast.102) | data formatting | bytes 3145728 | tf_op jit(solution)/shard_map/reshape | solution.py:36
  37.5 0.0 copy-start.2
  37.5 0.0 all-to-all-done
  37.5 13.5 %all-to-all-start.1 = ((bf16[256,16,1,2,96]{4,1,3,2,0:T(8,128)(2,1)}), bf16[256,16,1,2,96]{4,1,3,2,0:T(8,128)(2,1)S(1)}, u32[]{:S(2)}, u32[]{:S(2)}) async-start(bf16[256,16,1,2,96]{4,1,3,2,0:T(8,128)(2,1)} %copy.44), calls=%async_computation.1 | async-start | bytes 4194304 | tf_op jit(solution)/shard_map/all_to_all | solution.py:37
  51.0 0.0 copy-done.2
  51.0 0.3 slice_reduce_fusion.2
  51.3 0.1 mul.73
  51.4 0.1 mul.78
  51.5 0.1 mul.83
  51.5 0.1 fusion.20
  51.7 0.1 div.15
  51.7 11.5 %multiply_convert_fusion.1 = (bf16[512,1024]{1,0:T(8,128)(2,1)S(1)}, bf16[512,1024]{1,0:T(8,128)(2,1)S(1)}) fusion(f32[1024]{0:T(1024)S(1)} %div.15, s32[1024]{0:T(1024)S(1)} %mul.83, s32[512]{0:T(512)S(1)} %bitcast.108, s32[1024]{0:T(1024)S(1)} %mul.78, s32[512]{0:T(512)S(1)} %bitcast.109, s32[1024]{0:T(1024)S(1)} %mul.73, s32[512]{0:T(512)S(1)} %bitcast.107), kind=kLoop, calls=%fused_computation.31 | loop fusion | flops 28835840 | bytes 2119680 | tf_op jit(solution)/shard_map/convert.4
  63.2 1.5 pad_maximum_fusion
  64.7 39.8 %all-to-all-done.1 = bf16[256,16,1,2,96]{4,1,3,2,0:T(8,128)(2,1)S(1)} async-done(((bf16[256,16,1,2,96]{4,1,3,2,0:T(8,128)(2,1)}), bf16[256,16,1,2,96]{4,1,3,2,0:T(8,128)(2,1)S(1)}, u32[]{:S(2)}, u32[]{:S(2)}) %all-to-all-start.1) | async-done | bytes 1572896 | tf_op jit(solution)/shard_map/all_to_all | solution.py:37
  104.5 0.0 copy-start
  104.5 1.3 copy-done
  105.8 2.0 %copy.45 = bf16[4,64,16,1,2,96]{5,2,1,4,0,3:T(8,128)(2,1)S(1)} copy(bf16[4,64,16,1,2,96]{5,2,4,0,1,3:T(8,128)(2,1)} %bitcast.100) | data formatting | bytes 3145728 | tf_op jit(solution)/shard_map/transpose | solution.py:14
  107.8 2.5 %copy.46 = bf16[1024,4,1,2,96]{0,4,3,1,2:T(8,128)(2,1)} copy(bf16[1024,4,1,2,96]{4,0,3,1,2:T(8,128)(2,1)S(1)} %bitcast.99) | data formatting | bytes 3145728 | tf_op jit(solution)/shard_map/transpose | solution.py:14
  110.3 3.9 %fusion.8 = f32[2,512,4,2,96]{1,4,3,2,0:T(8,128)S(1)} fusion(bf16[2,512,1024,1,1]{2,1,4,3,0:T(8,128)(2,1)} %bitcast.104, bf16[1024,4,1,2,96]{0,4,3,1,2:T(8,128)(2,1)} %copy.46), kind=kOutput, calls=%fused_computation.32 | convolution fusion | flops 1610612736 | bytes 6815744 | tf_op jit(solution)/shard_map/dot_general | solution.py:57
  114.1 0.1 fusion.17
  114.2 0.1 fusion.18
  114.3 0.1 pad_maximum_fusion.3
  114.4 0.0 copy-start.1
  114.4 1.4 copy.49
  115.9 4.9 %all-to-all-start.2 = ((bf16[512,4,2,96]{3,1,2,0:T(4,128)(2,1)}), bf16[512,4,2,96]{3,1,2,0:T(4,128)(2,1)S(1)}, u32[]{:S(2)}, u32[]{:S(2)}) async-start(bf16[512,4,2,96]{3,1,2,0:T(4,128)(2,1)} %copy.49), calls=%async_computation.2 | async-start | bytes 2097152 | tf_op jit(solution)/shard_map/all_to_all | solution.py:81
  120.8 0.0 copy-done.1
  120.9 0.1 copy.64
  121.0 0.1 copy.65
  121.1 33.1 %all-to-all-done.2 = bf16[512,4,2,96]{3,1,2,0:T(4,128)(2,1)S(1)} async-done(((bf16[512,4,2,96]{3,1,2,0:T(4,128)(2,1)}), bf16[512,4,2,96]{3,1,2,0:T(4,128)(2,1)S(1)}, u32[]{:S(2)}, u32[]{:S(2)}) %all-to-all-start.2) | async-done | bytes 786464 | tf_op jit(solution)/shard_map/all_to_all | solution.py:81
  154.2 0.1 copy.69
  154.4 0.3 copy.60
  154.7 1.8 %reshape.102 = bf16[8,4,2,6,1024]{4,3,1,0,2:T(8,128)(2,1)S(1)} reshape(bf16[8,4,2,64,96]{4,3,1,0,2:T(8,128)(2,1)S(1)} %copy.60) | data formatting | bytes 1572864 | tf_op jit(solution)/shard_map/reshape | solution.py:105
  156.4 0.6 fusion.16
  157.0 0.6 fusion.15
  157.6 0.6 fusion.11
  158.2 0.6 fusion.10
  158.8 0.2 pad_maximum_fusion.2
  159.0 2.4 %copy.56 = f32[8,4,2,6,1024]{4,2,3,1,0:T(2,128)} copy(f32[8,4,2,6,1024]{4,3,1,0,2:T(8,128)S(1)} %pad_maximum_fusion.2) | data formatting | bytes 3145728 | tf_op jit(solution)/shard_map/stack | solution.py:77
  (2 shorter events, 0.0 us)
Async XLA Ops:
  1.4 36.1 %all-to-all-start = ((s32[64,4,16]{2,1,0:T(4,128)}), s32[64,4,16]{2,1,0:T(4,128)S(1)}, u32[]{:S(2)}, u32[]{:S(2)}) async-start(s32[64,4,16]{2,1,0:T(4,128)} %broadcast_in_dim.5), calls=%async_computation | async-start | bytes 262144 | tf_op jit(solution)/shard_map/all_to_all | solution.py:19
  37.5 13.5 %copy-start.2 = (s32[3,512]{1,0:T(4,128)S(1)}, s32[3,512]{1,0:T(4,128)}, u32[]{:S(2)}) copy-start(s32[3,512]{1,0:T(4,128)} %param.8) | copy-start | bytes 18436
  37.5 67.0 %all-to-all-start.1 = ((bf16[256,16,1,2,96]{4,1,3,2,0:T(8,128)(2,1)}), bf16[256,16,1,2,96]{4,1,3,2,0:T(8,128)(2,1)S(1)}, u32[]{:S(2)}, u32[]{:S(2)}) async-start(bf16[256,16,1,2,96]{4,1,3,2,0:T(8,128)(2,1)} %copy.44), calls=%async_computation.1 | async-start | bytes 4194304 | tf_op jit(solution)/shard_map/all_to_all | solution.py:37
  104.5 1.3 copy-start
  114.4 6.4 %copy-start.1 = (f32[8,2,6,6]{0,1,3,2:T(2,128)S(1)}, f32[8,2,6,6]{0,1,3,2:T(2,128)}, u32[]{:S(2)}) copy-start(f32[8,2,6,6]{0,1,3,2:T(2,128)} %param.9) | copy-start | bytes 6916
  115.9 38.4 %all-to-all-start.2 = ((bf16[512,4,2,96]{3,1,2,0:T(4,128)(2,1)}), bf16[512,4,2,96]{3,1,2,0:T(4,128)(2,1)S(1)}, u32[]{:S(2)}, u32[]{:S(2)}) async-start(bf16[512,4,2,96]{3,1,2,0:T(4,128)(2,1)} %copy.49), calls=%async_computation.2 | async-start | bytes 2097152 | tf_op jit(solution)/shard_map/all_to_all | solution.py:81
where the time goes:
time: 162 us; the launch traced here: 161 us
  waiting for transfers between devices  72.9 us (45%)
  local copies, waits for them, and re-layouts  34.9 us (22%)
  starting transfers between devices  32.3 us (20%)
  other arithmetic  14.8 us (9%)
  matrix products  6.18 us (4%)
    all_to_all x1, waiting for transfers between devices, joined_exchange(): tiles = lax.all_to_all(tiles, axis, split_axis=0, concat_axis=0, tiled=True)  39.8 us
    all_to_all x1, waiting for transfers between devices, to_owners(): lax.all_to_all(all_points.astype(jnp.bfloat16), 'rp', split_axis=0, conca...  33.1 us
    all_to_all x1, starting transfers between devices, from_everyone(): lax.all_to_all(jnp.broadcast_to(x[None], (peers, *x.shape)), axis, 0, 0,...  13.9 us
    all_to_all x1, starting transfers between devices, joined_exchange(): tiles = lax.all_to_all(tiles, axis, split_axis=0, concat_axis=0, tiled=True)  13.5 us
    another operation x1, other arithmetic  11.5 us
    reshape x2, local copies, waits for them, and re-layouts, per_device(): coupling.reshape(local_rp, local_re, parts, mode_count, re_count, pair_sh...  6.25 us
    all_to_all x1, starting transfers between devices, to_owners(): lax.all_to_all(all_points.astype(jnp.bfloat16), 'rp', split_axis=0, conca...  4.92 us
    transpose x1, local copies, waits for them, and re-layouts, per_device(): reordered = jnp.swapaxes(reordered, 3, 4)  4.86 us
  transfers between devices with their start and end apart: 3, of which 2 were waited for; matrix products, arithmetic and copies ran while one was open for 22% of the time, Pallas kernels for 0%

commit v1 on v0

v1 whole, which is shorter than its diff:
```python
import math

import jax
import jax.numpy as jnp
from jax import lax
from jax.experimental import pallas as pl
from jax.experimental.pallas import tpu as pltpu
from jax.sharding import Mesh, PartitionSpec as P

QGRID = 16
PLANE = ("y", "x", "core")
EVERY = ("y", "x", "zh", "core", "re")
DATA_ROWS = 192
ROWS = 200


def fetch_kernel(source, out, sems):
    for m in range(6):
        @pl.loop(0, 32)
        def _(b):
            pltpu.make_async_copy(
                source.at[:, m, :, pl.ds(pl.multiple_of(b * 128, 128), 128)],
                out.at[m, b],
                sems.at[m],
            ).start()
    for m in range(6):
        pltpu.make_async_copy(out.at[m], out.at[m], sems.at[m]).wait()


def fetch(coupling):
    return pl.pallas_call(
        fetch_kernel,
        out_shape=pltpu.VMEM((6, 32, 16, 2, 128), jnp.bfloat16),
        in_specs=[pl.BlockSpec(memory_space=pl.ANY)],
        out_specs=pl.BlockSpec(memory_space=pltpu.VMEM),
        scratch_shapes=[pltpu.SemaphoreType.DMA((6,))],
        name="fetch",
    )(coupling)


def pack_kernel(place, blocks, coords, degeneracy, out, lattice):
    lane = lax.broadcasted_iota(jnp.int32, (16, 128), 1)
    row = lax.broadcasted_iota(jnp.int32, (16, 128), 0)
    spread = (lane == place[0] * 32 + 2 * row) | (lane == place[0] * 32 + 2 * row + 1)
    spread = spread.astype(jnp.float32).astype(jnp.bfloat16)
    lattice[...] = jnp.zeros_like(lattice)
    lattice[0:3, :] = jnp.dot(
        coords[...].astype(jnp.float32).astype(jnp.bfloat16), spread, preferred_element_type=jnp.float32
    )
    lattice[3:4, :] = jnp.dot(
        degeneracy[...].astype(jnp.float32).astype(jnp.bfloat16), spread, preferred_element_type=jnp.float32
    )
    mine = lattice[...].astype(jnp.bfloat16)

    @pl.loop(0, 8)
    def _(pair):
        for m in range(6):
            for half in range(2):
                a = blocks[m, 16 * half + pair]
                b = blocks[m, 16 * half + 8 + pair]
                at = pl.ds((m % 3 * 2 + half) * 32, 32)
                out[4 * pair + m // 3, at, :] = jnp.concatenate([a[:, :64], b[:, :64]], axis=1)
                out[4 * pair + 2 + m // 3, at, :] = jnp.concatenate([a[:, 64:], b[:, 64:]], axis=1)
        for u in range(4):
            out[4 * pair + u, DATA_ROWS:ROWS, :] = mine


def pack(place, blocks, coords, degeneracy):
    vmem = pl.BlockSpec(memory_space=pltpu.VMEM)
    return pl.pallas_call(
        pack_kernel,
        out_shape=pltpu.VMEM((32, ROWS, 128), jnp.bfloat16),
        in_specs=[pl.BlockSpec(memory_space=pltpu.SMEM), vmem, vmem, vmem],
        out_specs=vmem,
        scratch_shapes=[pltpu.VMEM((8, 128), jnp.float32)],
        name="pack",
    )(place, blocks, coords, degeneracy)


def combine_kernel(received, points, out, table):
    lane = lax.broadcasted_iota(jnp.int32, (512, 128), 1)
    odd = lane & 1
    position = lax.broadcasted_iota(jnp.int32, (1, 128), 1)
    cosines = jnp.zeros((1, 128), jnp.float32)
    for i in range(QGRID):
        value = math.cos(2.0 * math.pi * i / QGRID) if i % 8 != 4 else 0.0
        cosines = jnp.where(position == i, value, cosines)
    cosines = jnp.broadcast_to(cosines, (512, 128))
    q = points[...].astype(jnp.bfloat16)

    @pl.loop(0, 8)
    def _(k):
        rows = received[pl.ds(4 * k, 4), DATA_ROWS:ROWS, :].astype(jnp.float32)
        rows = rows[0] + rows[1] + rows[2] + rows[3]
        weights = 1.0 / rows[3:4, :]
        turns = jnp.dot(q, rows.astype(jnp.bfloat16), preferred_element_type=jnp.float32).astype(jnp.int32)
        first = jnp.take_along_axis(cosines, (turns + 4 * odd) & (QGRID - 1), axis=1)
        second = jnp.take_along_axis(cosines, (turns + 12 - 12 * odd) & (QGRID - 1), axis=1)
        at = pl.ds(pl.multiple_of(k * 128, 128), 128)
        table[0:512, at] = (first * weights).astype(jnp.bfloat16)
        table[512:1024, at] = (second * weights).astype(jnp.bfloat16)

    low = lax.broadcasted_iota(jnp.int32, (512, 128), 1) < 64

    @pl.loop(0, 3)
    def _(m):
        at = pl.multiple_of(m * 64, 64)
        columns = jnp.concatenate(
            [
                received[:, pl.ds(at, 32), :].reshape(1024, 128),
                received[:, pl.ds(at + 32, 32), :].reshape(1024, 128),
            ],
            axis=1,
        )
        product = jnp.dot(table[...], columns, preferred_element_type=jnp.float32)
        rows = pl.ds(pl.multiple_of(m * 8, 8), 8)
        for half in range(2):
            real = product[0:512, 128 * half : 128 * half + 128]
            imag = product[512:1024, 128 * half : 128 * half + 128]
            near = jnp.where(low, real, pltpu.roll(imag, 64, 1))
            far = jnp.where(low, pltpu.roll(real, 64, 1), imag)
            out[:, 2 * half, rows, :] = near.reshape(64, 8, 128).astype(jnp.bfloat16)
            out[:, 2 * half + 1, rows, :] = far.reshape(64, 8, 128).astype(jnp.bfloat16)


def combine(received, points):
    vmem = pl.BlockSpec(memory_space=pltpu.VMEM)
    return pl.pallas_call(
        combine_kernel,
        out_shape=pltpu.VMEM((64, 4, 24, 128), jnp.bfloat16),
        in_specs=[vmem, vmem],
        out_specs=vmem,
        scratch_shapes=[pltpu.VMEM((1024, 1024), jnp.bfloat16)],
        name="combine",
    )(received, points)


def rotate_kernel(summed, eigvec, out, factors):
    for i in range(72):
        factors[i] = jnp.broadcast_to(eigvec[:, i : i + 1], (8, 128))
    low = lax.broadcasted_iota(jnp.int32, (8, 128), 1) < 64

    @pl.loop(0, 32)
    def _(step):
        e = step // 8
        block = step % 8

        def piece(h, k):
            rows = pl.ds(k % 3 * 8, 8)
            return summed[2 * block + h, 0, k // 3, e, rows, :].astype(jnp.float32) + summed[
                2 * block + h, 1, k // 3, e, rows, :
            ].astype(jnp.float32)

        real, imag = [], []
        for k in range(6):
            left, right = piece(0, k), piece(1, k)
            real.append(jnp.where(low, left, pltpu.roll(right, 64, 1)))
            imag.append(jnp.where(low, pltpu.roll(left, 64, 1), right))
        for n in range(6):
            real_out = jnp.zeros((8, 128), jnp.float32)
            imag_out = jnp.zeros((8, 128), jnp.float32)
            for k in range(6):
                vec_real = factors[k * 6 + n]
                vec_imag = factors[36 + k * 6 + n]
                real_out = real_out + real[k] * vec_real - imag[k] * vec_imag
                imag_out = imag_out + real[k] * vec_imag + imag[k] * vec_real
            at = e * 96 + n * 16 + block * 2
            out[pl.ds(at, 8, stride=384), :] = real_out
            out[pl.ds(at + 1, 8, stride=384), :] = imag_out


def rotate(summed, eigvec):
    vmem = pl.BlockSpec(memory_space=pltpu.VMEM)
    return pl.pallas_call(
        rotate_kernel,
        out_shape=jax.ShapeDtypeStruct((3072, 128), jnp.float32),
        in_specs=[vmem, vmem],
        out_specs=vmem,
        scratch_shapes=[pltpu.VMEM((72, 8, 128), jnp.float32)],
        name="rotate",
    )(summed, eigvec)


def per_device(coupling, rp_coords, degeneracy, qpoints, eigvec):
    place = (lax.axis_index(PLANE) % 4).astype(jnp.int32).reshape(1)
    points = jnp.pad(qpoints.T.astype(jnp.float32), ((0, 0), (0, 5)))
    vectors = eigvec.reshape(8, 72)
    blocks = fetch(coupling.reshape(16, 2, 6, 4096).transpose(0, 2, 1, 3)).reshape(6, 32, 32, 128)
    message = pack(place, blocks, rp_coords, degeneracy.reshape(1, 16))
    received = lax.all_to_all(message, PLANE, 0, 0, tiled=True)
    partial = combine(received, points).reshape(256, 24, 128)
    summed = lax.all_to_all(partial, EVERY, 0, 0, tiled=True)
    result = rotate(summed.reshape(16, 2, 2, 4, 24, 128), vectors)
    return result.reshape(8, 4, 6, 8, 2, 128).transpose(0, 1, 4, 2, 3, 5).reshape(8, 4, 2, 6, 1024)


def solution(mesh):
    rp = ("y", "x", "zh", "core")
    inner = Mesh(mesh.devices.reshape(4, 4, 2, 2, 4), EVERY)
    return jax.shard_map(
        per_device,
        mesh=inner,
        in_specs=(P(rp, "re", None, None, None), P(None, rp), P(rp), P(), P(rp, None, None, None)),
        out_specs=P(rp, None, None, None, "re"),
        check_vma=False,
    )
```

time: 162 us -> 114 us (0.70)
  the two profiles are of different devices: /device:TPU:33 before, /device:TPU:1 now
where the time goes in v1:
time: 114 us
  waiting for transfers between devices  65.4 us (57%)
  Pallas kernels  23 us (20%)
  starting transfers between devices  20 us (18%)
  local copies, waits for them, and re-layouts  5.19 us (5%)
    all_to_all x1, waiting for transfers between devices, per_device(): summed = lax.all_to_all(partial, EVERY, 0, 0, tiled=True)  42.7 us
    all_to_all x1, waiting for transfers between devices, per_device(): received = lax.all_to_all(message, PLANE, 0, 0, tiled=True)  22.7 us
    all_to_all x1, starting transfers between devices, per_device(): summed = lax.all_to_all(partial, EVERY, 0, 0, tiled=True)  11.3 us
    pallas_call x1, Pallas kernels, combine(): pl.pallas_call(combine_kernel, out_shape=pltpu.VMEM((64, 4, 24, 128), jnp...  9.44 us
    all_to_all x1, starting transfers between devices, per_device(): received = lax.all_to_all(message, PLANE, 0, 0, tiled=True)  8.71 us
    pallas_call x1, Pallas kernels, rotate(): pl.pallas_call(rotate_kernel, out_shape=jax.ShapeDtypeStruct((3072, 128),...  7.27 us
    pallas_call x1, Pallas kernels, pack(): pl.pallas_call(pack_kernel, out_shape=pltpu.VMEM((32, ROWS, 128), jnp.bfl...  3.69 us
    unnamed x11, local copies, waits for them, and re-layouts  3.63 us
  transfers between devices with their start and end apart: 2, of which 2 were waited for; matrix products, arithmetic and copies ran while one was open for 2% of the time, Pallas kernels for 0%

profile of v1, /device:TPU:1, one launch (start us, length us, event | category | flops | bytes accessed | tf_op | source)
XLA Modules:
  0.0 113.6 jit_solution(6576963613828632410)
XLA Ops:
  0.0 2.6 %fetch.1 = bf16[6,32,16,2,128]{4,3,2,1,0:T(2,128)(2,1)S(1)} custom-call(bf16[16,6,2,4096]{3,2,1,0:T(2,128)(2,1)} %bitcast.16), custom_call_target="tpu_custom_call" | custom-call | tf_op jit(solution)/shard_map/fetch/pallas_call | solution.py:31
  2.6 0.0 copy-start
  2.6 1.1 copy-done
  3.7 3.7 %pack.1 = bf16[32,200,128]{2,1,0:T(8,128)(2,1)} custom-call(s32[1]{0:T(128)} %bitcast.place, bf16[6,32,32,128]{3,2,1,0:T(8,128)(2,1)} %bitcast.14, s32[3,16]{1,0:T(4,128)} %coords.1, s32[1,16]{1,0:T(1,128)} %bitcast.18), custom_call_target="tpu_custom_call" | custom-call | tf_op jit(solution)/shard_map/pack/pallas_call | solution.py:70
  7.4 0.0 copy-start.4
  7.4 8.7 %all-to-all-start = ((bf16[32,200,128]{2,1,0:T(8,128)(2,1)}), bf16[32,200,128]{2,1,0:T(8,128)(2,1)S(1)}, u32[]{:S(2)}, u32[]{:S(2)}) async-start(bf16[32,200,128]{2,1,0:T(8,128)(2,1)} %pack.1), calls=%async_computation | async-start | bytes 3276800 | tf_op jit(solution)/shard_map/all_to_all | solution.py:190
  16.1 0.0 copy-done.4
  16.2 0.1 copy.9
  16.3 0.7 pad.4.points
  17.1 22.7 %all-to-all-done.received = bf16[32,200,128]{2,1,0:T(8,128)(2,1)S(1)} async-done(((bf16[32,200,128]{2,1,0:T(8,128)(2,1)}), bf16[32,200,128]{2,1,0:T(8,128)(2,1)S(1)}, u32[]{:S(2)}, u32[]{:S(2)}) %all-to-all-start) | async-done | bytes 1638432 | tf_op jit(solution)/shard_map/all_to_all | solution.py:190
  39.7 0.0 copy-start.1
  39.7 1.2 %copy-done.1 = bf16[32,200,128]{2,1,0:T(8,128)(2,1)} copy-done((bf16[32,200,128]{2,1,0:T(8,128)(2,1)}, bf16[32,200,128]{2,1,0:T(8,128)(2,1)S(1)}, u32[]{:S(2)}) %copy-start.1) | copy-done | bytes 1638424
  40.9 9.4 %combine.1 = bf16[64,4,24,128]{3,2,1,0:T(8,128)(2,1)} custom-call(bf16[32,200,128]{2,1,0:T(8,128)(2,1)} %copy-done.1, f32[512,8]{1,0:T(8,128)} %pad.4.points), custom_call_target="tpu_custom_call" | custom-call | tf_op jit(solution)/shard_map/combine/pallas_call | solution.py:128
  50.3 0.0 copy-start.3
  50.3 11.3 %all-to-all-start.1 = ((bf16[256,24,128]{2,1,0:T(8,128)(2,1)}), bf16[256,24,128]{2,1,0:T(8,128)(2,1)S(1)}, u32[]{:S(2)}, u32[]{:S(2)}) async-start(bf16[256,24,128]{2,1,0:T(8,128)(2,1)} %bitcast.6), calls=%async_computation.1 | async-start | bytes 3145728 | tf_op jit(solution)/shard_map/all_to_all | solution.py:192
  61.6 0.0 copy-done.3
  61.6 0.2 copy.10
  61.8 0.7 reshape.33.eigvec
  62.5 42.7 %all-to-all-done.1 = bf16[256,24,128]{2,1,0:T(8,128)(2,1)S(1)} async-done(((bf16[256,24,128]{2,1,0:T(8,128)(2,1)}), bf16[256,24,128]{2,1,0:T(8,128)(2,1)S(1)}, u32[]{:S(2)}, u32[]{:S(2)}) %all-to-all-start.1) | async-done | bytes 1572896 | tf_op jit(solution)/shard_map/all_to_all | solution.py:192
  105.2 0.0 copy-start.2
  105.2 1.1 %copy-done.2 = bf16[256,24,128]{2,1,0:T(8,128)(2,1)} copy-done((bf16[256,24,128]{2,1,0:T(8,128)(2,1)}, bf16[256,24,128]{2,1,0:T(8,128)(2,1)S(1)}, u32[]{:S(2)}) %copy-start.2) | copy-done | bytes 1572888
  106.3 7.3 %rotate.1 = f32[3072,128]{1,0:T(8,128)} custom-call(bf16[16,2,2,4,24,128]{5,4,3,2,1,0:T(8,128)(2,1)} %bitcast.15, f32[8,72]{1,0:T(8,128)} %reshape.33.eigvec), custom_call_target="tpu_custom_call" | custom-call | tf_op jit(solution)/shard_map/rotate/pallas_call | solution.py:174
  (1 shorter events, 0.0 us)
Async XLA Ops:
  2.6 1.1 %copy-start = (bf16[6,32,16,2,128]{4,3,2,1,0:T(2,128)(2,1)}, bf16[6,32,16,2,128]{4,3,2,1,0:T(2,128)(2,1)S(1)}, u32[]{:S(2)}) copy-start(bf16[6,32,16,2,128]{4,3,2,1,0:T(2,128)(2,1)S(1)} %fetch.1) | copy-start | bytes 4718596
  7.4 8.7 %copy-start.4 = (s32[3,512]{1,0:T(4,128)S(1)}, s32[3,512]{1,0:T(4,128)}, u32[]{:S(2)}) copy-start(s32[3,512]{1,0:T(4,128)} %param.8) | copy-start | bytes 18436
  7.4 32.3 %all-to-all-start = ((bf16[32,200,128]{2,1,0:T(8,128)(2,1)}), bf16[32,200,128]{2,1,0:T(8,128)(2,1)S(1)}, u32[]{:S(2)}, u32[]{:S(2)}) async-start(bf16[32,200,128]{2,1,0:T(8,128)(2,1)} %pack.1), calls=%async_computation | async-start | bytes 3276800 | tf_op jit(solution)/shard_map/all_to_all | solution.py:190
  39.7 1.2 %copy-start.1 = (bf16[32,200,128]{2,1,0:T(8,128)(2,1)}, bf16[32,200,128]{2,1,0:T(8,128)(2,1)S(1)}, u32[]{:S(2)}) copy-start(bf16[32,200,128]{2,1,0:T(8,128)(2,1)S(1)} %all-to-all-done.received) | copy-start | bytes 4915204
  50.3 11.3 %copy-start.3 = (f32[8,2,6,6]{0,1,3,2:T(2,128)S(1)}, f32[8,2,6,6]{0,1,3,2:T(2,128)}, u32[]{:S(2)}) copy-start(f32[8,2,6,6]{0,1,3,2:T(2,128)} %param.9) | copy-start | bytes 6916
  50.3 54.8 %all-to-all-start.1 = ((bf16[256,24,128]{2,1,0:T(8,128)(2,1)}), bf16[256,24,128]{2,1,0:T(8,128)(2,1)S(1)}, u32[]{:S(2)}, u32[]{:S(2)}) async-start(bf16[256,24,128]{2,1,0:T(8,128)(2,1)} %bitcast.6), calls=%async_computation.1 | async-start | bytes 3145728 | tf_op jit(solution)/shard_map/all_to_all | solution.py:192
  105.2 1.1 %copy-start.2 = (bf16[256,24,128]{2,1,0:T(8,128)(2,1)}, bf16[256,24,128]{2,1,0:T(8,128)(2,1)S(1)}, u32[]{:S(2)}) copy-start(bf16[256,24,128]{2,1,0:T(8,128)(2,1)S(1)} %all-to-all-done.1) | copy-start | bytes 4718596

commit v2 on v1

--- a/solution.py
+++ b/solution.py
@@ -16,7 +16,7 @@
 
 def fetch_kernel(source, out, sems):
     for m in range(6):
-        @pl.loop(0, 32)
+        @pl.loop(0, 32, unroll=8)
         def _(b):
             pltpu.make_async_copy(
                 source.at[:, m, :, pl.ds(pl.multiple_of(b * 128, 128), 128)],
@@ -52,7 +52,7 @@
     )
     mine = lattice[...].astype(jnp.bfloat16)
 
-    @pl.loop(0, 8)
+    @pl.loop(0, 8, unroll=2)
     def _(pair):
         for m in range(6):
             for half in range(2):
@@ -77,28 +77,34 @@
     )(place, blocks, coords, degeneracy)
 
 
-def combine_kernel(received, points, out, table):
-    lane = lax.broadcasted_iota(jnp.int32, (512, 128), 1)
-    odd = lane & 1
-    position = lax.broadcasted_iota(jnp.int32, (1, 128), 1)
-    cosines = jnp.zeros((1, 128), jnp.float32)
-    for i in range(QGRID):
-        value = math.cos(2.0 * math.pi * i / QGRID) if i % 8 != 4 else 0.0
-        cosines = jnp.where(position == i, value, cosines)
-    cosines = jnp.broadcast_to(cosines, (512, 128))
-    q = points[...].astype(jnp.bfloat16)
-
-    @pl.loop(0, 8)
-    def _(k):
-        rows = received[pl.ds(4 * k, 4), DATA_ROWS:ROWS, :].astype(jnp.float32)
+def combine_kernel(received, points, out, table, lattice):
+    shift = 4.0 * (lax.broadcasted_iota(jnp.int32, (1, 128), 1) & 1).astype(jnp.float32)
+    for k in range(8):
+        at = slice(k * 128, k * 128 + 128)
+        rows = received[4 * k : 4 * k + 4, DATA_ROWS:ROWS, :].astype(jnp.float32)
         rows = rows[0] + rows[1] + rows[2] + rows[3]
-        weights = 1.0 / rows[3:4, :]
-        turns = jnp.dot(q, rows.astype(jnp.bfloat16), preferred_element_type=jnp.float32).astype(jnp.int32)
-        first = jnp.take_along_axis(cosines, (turns + 4 * odd) & (QGRID - 1), axis=1)
-        second = jnp.take_along_axis(cosines, (turns + 12 - 12 * odd) & (QGRID - 1), axis=1)
-        at = pl.ds(pl.multiple_of(k * 128, 128), 128)
-        table[0:512, at] = (first * weights).astype(jnp.bfloat16)
-        table[512:1024, at] = (second * weights).astype(jnp.bfloat16)
+        lattice[0:3, at] = rows[0:3]
+        lattice[3:4, at] = 1.0 / rows[3:4]
+    c1, c2, c3 = (math.cos(2.0 * math.pi * i / QGRID) for i in (1, 2, 3))
+
+    @pl.loop(0, 16)
+    def _(chunk):
+        q = points[pl.ds(pl.multiple_of(chunk * 32, 32), 32), :]
+        q0, q1, q2 = (jnp.broadcast_to(q[:, d : d + 1], (32, 128)) for d in range(3))
+        for k in range(8):
+            at = slice(k * 128, k * 128 + 128)
+            turns = q0 * lattice[0:1, at] + q1 * lattice[1:2, at] + (q2 * lattice[2:3, at] + shift)
+            turns = turns.astype(jnp.int32)
+            bit0, bit1, bit2, bit3 = ((turns & b) != 0 for b in (1, 2, 4, 8))
+            cosine = jnp.where(bit1, jnp.where(bit0, c3, c2), jnp.where(bit0, c1, 1.0))
+            sine = jnp.where(bit1, jnp.where(bit0, c1, c2), jnp.where(bit0, c3, 0.0))
+            weight = jnp.broadcast_to(lattice[3:4, at], (32, 128))
+            sine_weight = jnp.where(bit3, -weight, weight)
+            cosine_weight = jnp.where(bit2, -sine_weight, sine_weight)
+            first = jnp.where(bit2, sine, cosine) * cosine_weight
+            second = jnp.where(bit2, cosine, sine) * sine_weight
+            table[pl.ds(pl.multiple_of(chunk * 32, 32), 32), at] = first.astype(jnp.bfloat16)
+            table[pl.ds(pl.multiple_of(512 + chunk * 32, 32), 32), at] = second.astype(jnp.bfloat16)
 
     low = lax.broadcasted_iota(jnp.int32, (512, 128), 1) < 64
 
@@ -130,43 +136,55 @@
         out_shape=pltpu.VMEM((64, 4, 24, 128), jnp.bfloat16),
         in_specs=[vmem, vmem],
         out_specs=vmem,
-        scratch_shapes=[pltpu.VMEM((1024, 1024), jnp.bfloat16)],
+        scratch_shapes=[pltpu.VMEM((1024, 1024), jnp.bfloat16), pltpu.VMEM((8, 1024), jnp.float32)],
         name="combine",
     )(received, points)
 
 
-def rotate_kernel(summed, eigvec, out, factors):
+def rotate_kernel(summed, eigvec, out, factors, result, sem):
     for i in range(72):
         factors[i] = jnp.broadcast_to(eigvec[:, i : i + 1], (8, 128))
     low = lax.broadcasted_iota(jnp.int32, (8, 128), 1) < 64
 
-    @pl.loop(0, 32)
-    def _(step):
-        e = step // 8
-        block = step % 8
-
+    @pl.loop(0, 4)
+    def _(e):
         def piece(h, k):
-            rows = pl.ds(k % 3 * 8, 8)
-            return summed[2 * block + h, 0, k // 3, e, rows, :].astype(jnp.float32) + summed[
-                2 * block + h, 1, k // 3, e, rows, :
+            rows = slice(k % 3 * 8, k % 3 * 8 + 8)
+            return summed[h, 0, k // 3, e, rows, :].astype(jnp.float32) + summed[
+                h, 1, k // 3, e, rows, :
             ].astype(jnp.float32)
 
-        real, imag = [], []
-        for k in range(6):
-            left, right = piece(0, k), piece(1, k)
-            real.append(jnp.where(low, left, pltpu.roll(right, 64, 1)))
-            imag.append(jnp.where(low, pltpu.roll(left, 64, 1), right))
-        for n in range(6):
-            real_out = jnp.zeros((8, 128), jnp.float32)
-            imag_out = jnp.zeros((8, 128), jnp.float32)
-            for k in range(6):
-                vec_real = factors[k * 6 + n]
-                vec_imag = factors[36 + k * 6 + n]
-                real_out = real_out + real[k] * vec_real - imag[k] * vec_imag
-                imag_out = imag_out + real[k] * vec_imag + imag[k] * vec_real
-            at = e * 96 + n * 16 + block * 2
-            out[pl.ds(at, 8, stride=384), :] = real_out
-            out[pl.ds(at + 1, 8, stride=384), :] = imag_out
+        @pl.loop(0, 4, unroll=4)
+        def _(step):
+            blocks = (2 * step, 2 * step + 1)
+            real, imag = {}, {}
+            for i, block in enumerate(blocks):
+                for k in range(6):
+                    left, right = piece(2 * block, k), piece(2 * block + 1, k)
+                    real[i, k] = jnp.where(low, left, pltpu.roll(right, 64, 1))
+                    imag[i, k] = jnp.where(low, pltpu.roll(left, 64, 1), right)
+            for n in range(6):
+                totals = {}
+                for k in range(6):
+                    vec_real = factors[k * 6 + n]
+                    vec_imag = factors[36 + k * 6 + n]
+                    for i in range(2):
+                        terms = (
+                            real[i, k] * vec_real - imag[i, k] * vec_imag,
+                            real[i, k] * vec_imag + imag[i, k] * vec_real,
+                        )
+                        for part in range(2):
+                            totals[i, part] = totals[i, part] + terms[part] if k else terms[part]
+                for i, block in enumerate(blocks):
+                    for part in range(2):
+                        at = e * 96 + n * 16 + block * 2 + part
+                        result[pl.ds(at, 8, stride=384), :] = totals[i, part]
+
+        for q in range(8):
+            at = pl.ds(pl.multiple_of(q * 384 + e * 96, 32), 96)
+            pltpu.make_async_copy(result.at[at], out.at[at], sem).start()
+
+    pltpu.make_async_copy(result, out, sem).wait()
 
 
 def rotate(summed, eigvec):
@@ -175,10 +193,18 @@
         rotate_kernel,
         out_shape=jax.ShapeDtypeStruct((3072, 128), jnp.float32),
         in_specs=[vmem, vmem],
-        out_specs=vmem,
-        scratch_shapes=[pltpu.VMEM((72, 8, 128), jnp.float32)],
+        out_specs=pl.BlockSpec(memory_space=pl.ANY),
+        scratch_shapes=[
+            pltpu.VMEM((72, 8, 128), jnp.float32),
+            pltpu.VMEM((3072, 128), jnp.float32),
+            pltpu.SemaphoreType.DMA,
+        ],
         name="rotate",
     )(summed, eigvec)
+
+
+def on_chip(x):
+    return pltpu.with_memory_space_constraint(x, pltpu.VMEM)
 
 
 def per_device(coupling, rp_coords, degeneracy, qpoints, eigvec):
@@ -186,11 +212,11 @@
     points = jnp.pad(qpoints.T.astype(jnp.float32), ((0, 0), (0, 5)))
     vectors = eigvec.reshape(8, 72)
     blocks = fetch(coupling.reshape(16, 2, 6, 4096).transpose(0, 2, 1, 3)).reshape(6, 32, 32, 128)
-    message = pack(place, blocks, rp_coords, degeneracy.reshape(1, 16))
+    message = pack(place, on_chip(blocks), rp_coords, degeneracy.reshape(1, 16))
     received = lax.all_to_all(message, PLANE, 0, 0, tiled=True)
-    partial = combine(received, points).reshape(256, 24, 128)
+    partial = combine(on_chip(received), points).reshape(256, 24, 128)
     summed = lax.all_to_all(partial, EVERY, 0, 0, tiled=True)
-    result = rotate(summed.reshape(16, 2, 2, 4, 24, 128), vectors)
+    result = rotate(on_chip(summed.reshape(16, 2, 2, 4, 24, 128)), vectors)
     return result.reshape(8, 4, 6, 8, 2, 128).transpose(0, 1, 4, 2, 3, 5).reshape(8, 4, 2, 6, 1024)
 
 

time: 114 us -> 104 us (0.912)
  Pallas kernels: 23 us -> 16.2 us
  local copies, waits for them, and re-layouts: 5.19 us -> 1.71 us
    unnamed x11 -> x5, local copies, waits for them, and re-layouts: 3.63 us -> 0.16 us
    pallas_call x1, Pallas kernels: 7.27 us -> 3.99 us  [rotate(): pl.pallas_call(rotate_kernel, out_shape=jax.ShapeDtypeStruct((3072, 128),...]
    pallas_call x1, Pallas kernels: 9.44 us -> 7.91 us  [combine(): pl.pallas_call(combine_kernel, out_shape=pltpu.VMEM((64, 4, 24, 128), jnp...]
where the time goes in v2:
time: 104 us; the launch traced here: 103 us
  waiting for transfers between devices  65.4 us (63%)
  starting transfers between devices  20 us (19%)
  Pallas kernels  16.2 us (16%)
  local copies, waits for them, and re-layouts  1.71 us (2%)
    all_to_all x1, waiting for transfers between devices, per_device(): summed = lax.all_to_all(partial, EVERY, 0, 0, tiled=True)  42.7 us
    all_to_all x1, waiting for transfers between devices, per_device(): received = lax.all_to_all(message, PLANE, 0, 0, tiled=True)  22.7 us
    all_to_all x1, starting transfers between devices, per_device(): summed = lax.all_to_all(partial, EVERY, 0, 0, tiled=True)  11.3 us
    all_to_all x1, starting transfers between devices, per_device(): received = lax.all_to_all(message, PLANE, 0, 0, tiled=True)  8.71 us
    pallas_call x1, Pallas kernels, combine(): pl.pallas_call(combine_kernel, out_shape=pltpu.VMEM((64, 4, 24, 128), jnp...  7.91 us
    pallas_call x1, Pallas kernels, rotate(): pl.pallas_call(rotate_kernel, out_shape=jax.ShapeDtypeStruct((3072, 128),...  3.99 us
    pallas_call x1, Pallas kernels, pack(): pl.pallas_call(pack_kernel, out_shape=pltpu.VMEM((32, ROWS, 128), jnp.bfl...  2.67 us
  transfers between devices with their start and end apart: 2, of which 2 were waited for; matrix products, arithmetic and copies ran while one was open for 2% of the time, Pallas kernels for 0%

profile of v2, /device:TPU:1, one launch (start us, length us, event | category | flops | bytes accessed | tf_op | source)
XLA Modules:
  0.0 103.4 jit_solution(15933338237534034981)
XLA Ops:
  0.0 1.7 %fetch.1 = bf16[6,32,16,2,128]{4,3,2,1,0:T(2,128)(2,1)S(1)} custom-call(bf16[16,6,2,4096]{3,2,1,0:T(2,128)(2,1)} %bitcast.16), custom_call_target="tpu_custom_call" | custom-call | tf_op jit(solution)/shard_map/fetch/pallas_call | solution.py:31
  1.7 2.7 %pack.1 = bf16[32,200,128]{2,1,0:T(8,128)(2,1)} custom-call(s32[1]{0:T(128)} %bitcast.place, bf16[6,32,32,128]{3,2,1,0:T(8,128)(2,1)S(1)} %bitcast.15, s32[3,16]{1,0:T(4,128)} %coords.1, s32[1,16]{1,0:T(1,128)} %bitcast.18), custom_call_target="tpu_custom_call" | custom-call | tf_op jit(solution)/shard_map/pack/pallas_call | solution.py:70
  4.4 0.0 copy-start.1
  4.4 8.7 %all-to-all-start = ((bf16[32,200,128]{2,1,0:T(8,128)(2,1)}), bf16[32,200,128]{2,1,0:T(8,128)(2,1)S(1)}, u32[]{:S(2)}, u32[]{:S(2)}) async-start(bf16[32,200,128]{2,1,0:T(8,128)(2,1)} %pack.1), calls=%async_computation | async-start | bytes 3276800 | tf_op jit(solution)/shard_map/all_to_all | solution.py:216
  13.1 0.0 copy-done.1
  13.1 0.1 copy.9
  13.3 0.7 pad.4.points
  14.0 22.7 %all-to-all-done.received = bf16[32,200,128]{2,1,0:T(8,128)(2,1)S(1)} async-done(((bf16[32,200,128]{2,1,0:T(8,128)(2,1)}), bf16[32,200,128]{2,1,0:T(8,128)(2,1)S(1)}, u32[]{:S(2)}, u32[]{:S(2)}) %all-to-all-start) | async-done | bytes 1638432 | tf_op jit(solution)/shard_map/all_to_all | solution.py:216
  36.7 7.9 %combine.1 = bf16[64,4,24,128]{3,2,1,0:T(8,128)(2,1)} custom-call(bf16[32,200,128]{2,1,0:T(8,128)(2,1)S(1)} %all-to-all-done.received, f32[512,8]{1,0:T(8,128)} %pad.4.points), custom_call_target="tpu_custom_call" | custom-call | tf_op jit(solution)/shard_map/combine/pallas_call | solution.py:134
  44.6 0.0 copy-start
  44.6 11.3 %all-to-all-start.1 = ((bf16[256,24,128]{2,1,0:T(8,128)(2,1)}), bf16[256,24,128]{2,1,0:T(8,128)(2,1)S(1)}, u32[]{:S(2)}, u32[]{:S(2)}) async-start(bf16[256,24,128]{2,1,0:T(8,128)(2,1)} %bitcast.6), calls=%async_computation.1 | async-start | bytes 3145728 | tf_op jit(solution)/shard_map/all_to_all | solution.py:218
  55.9 0.0 copy-done
  55.9 0.2 copy.10
  56.0 0.7 reshape.33.eigvec
  56.7 42.7 %all-to-all-done.1 = bf16[256,24,128]{2,1,0:T(8,128)(2,1)S(1)} async-done(((bf16[256,24,128]{2,1,0:T(8,128)(2,1)}), bf16[256,24,128]{2,1,0:T(8,128)(2,1)S(1)}, u32[]{:S(2)}, u32[]{:S(2)}) %all-to-all-start.1) | async-done | bytes 1572896 | tf_op jit(solution)/shard_map/all_to_all | solution.py:218
  99.4 4.0 %rotate.1 = f32[3072,128]{1,0:T(8,128)} custom-call(bf16[16,2,2,4,24,128]{5,4,3,2,1,0:T(8,128)(2,1)S(1)} %bitcast.14, f32[8,72]{1,0:T(8,128)} %reshape.33.eigvec), custom_call_target="tpu_custom_call" | custom-call | tf_op jit(solution)/shard_map/rotate/pallas_call | solution.py:192
  (1 shorter events, 0.0 us)
Async XLA Ops:
  4.4 8.7 %copy-start.1 = (s32[3,512]{1,0:T(4,128)S(1)}, s32[3,512]{1,0:T(4,128)}, u32[]{:S(2)}) copy-start(s32[3,512]{1,0:T(4,128)} %param.8) | copy-start | bytes 18436
  4.4 32.3 %all-to-all-start = ((bf16[32,200,128]{2,1,0:T(8,128)(2,1)}), bf16[32,200,128]{2,1,0:T(8,128)(2,1)S(1)}, u32[]{:S(2)}, u32[]{:S(2)}) async-start(bf16[32,200,128]{2,1,0:T(8,128)(2,1)} %pack.1), calls=%async_computation | async-start | bytes 3276800 | tf_op jit(solution)/shard_map/all_to_all | solution.py:216
  44.6 11.3 %copy-start = (f32[8,2,6,6]{0,1,3,2:T(2,128)S(1)}, f32[8,2,6,6]{0,1,3,2:T(2,128)}, u32[]{:S(2)}) copy-start(f32[8,2,6,6]{0,1,3,2:T(2,128)} %param.9) | copy-start | bytes 6916
  44.6 54.8 %all-to-all-start.1 = ((bf16[256,24,128]{2,1,0:T(8,128)(2,1)}), bf16[256,24,128]{2,1,0:T(8,128)(2,1)S(1)}, u32[]{:S(2)}, u32[]{:S(2)}) async-start(bf16[256,24,128]{2,1,0:T(8,128)(2,1)} %bitcast.6), calls=%async_computation.1 | async-start | bytes 3145728 | tf_op jit(solution)/shard_map/all_to_all | solution.py:218

commit v3 on v2

v3 whole, which is shorter than its diff:
```python
import math

import jax
import jax.numpy as jnp
from jax import lax
from jax.experimental import pallas as pl
from jax.experimental.pallas import tpu as pltpu
from jax.sharding import Mesh, PartitionSpec as P

QGRID = 16
PLANE = ("y", "x", "core")
EVERY = ("y", "x", "zh", "core", "re")
DATA_ROWS = 192
ROWS = 200


def fetch_kernel(
    place, coupling, coords, degeneracy, qpoints, eigvec,
    blocks, mine, points, factors,
    coords_in, degeneracy_in, qpoints_in, eigvec_in, rows, columns, sems, small_sems,
):
    small = [
        pltpu.make_async_copy(source, target, small_sems.at[i])
        for i, (source, target) in enumerate(
            [(coords, coords_in), (degeneracy, degeneracy_in), (qpoints, qpoints_in), (eigvec, eigvec_in)]
        )
    ]
    for copy in small:
        copy.start()
    for m in range(6):
        @pl.loop(0, 32, unroll=8)
        def _(b):
            pltpu.make_async_copy(
                coupling.at[:, m, :, pl.ds(pl.multiple_of(b * 128, 128), 128)],
                blocks.at[m, b],
                sems.at[m],
            ).start()
    for copy in small:
        copy.wait()

    lane = lax.broadcasted_iota(jnp.int32, (16, 128), 1)
    row = lax.broadcasted_iota(jnp.int32, (16, 128), 0)
    spread = (lane == place[0] * 32 + 2 * row) | (lane == place[0] * 32 + 2 * row + 1)
    spread = spread.astype(jnp.float32).astype(jnp.bfloat16)
    rows[...] = jnp.zeros_like(rows)
    for at, values in ((slice(0, 3), coords_in), (slice(3, 4), degeneracy_in)):
        rows[at, 0:128] = jnp.dot(
            values[...].astype(jnp.float32).astype(jnp.bfloat16), spread, preferred_element_type=jnp.float32
        )
    mine[...] = rows[:, 0:128].astype(jnp.bfloat16)

    rows[...] = jnp.zeros_like(rows)
    rows[0:3, :] = qpoints_in[...].astype(jnp.float32)
    points[...] = jnp.transpose(rows[...])

    columns[...] = jnp.zeros_like(columns)
    for part in range(2):
        for k in range(6):
            for n in range(6):
                i = part * 36 + k * 6 + n
                columns[i : i + 1, 0:8] = eigvec_in[k, n, part : part + 1, :]
    turned = jnp.transpose(columns[...])
    for i in range(72):
        factors[i] = jnp.broadcast_to(turned[0:8, i : i + 1], (8, 128))

    for m in range(6):
        pltpu.make_async_copy(blocks.at[m], blocks.at[m], sems.at[m]).wait()


VMEM = pl.BlockSpec(memory_space=pltpu.VMEM)
LIMIT = 16 * 2**20


def on_chip(x):
    return pltpu.with_memory_space_constraint(x, pltpu.VMEM)


def fetch(place, coupling, coords, degeneracy, qpoints, eigvec):
    hbm = pl.BlockSpec(memory_space=pltpu.HBM)
    return pl.pallas_call(
        fetch_kernel,
        out_shape=(
            pltpu.VMEM((6, 32, 16, 2, 128), jnp.bfloat16),
            pltpu.VMEM((8, 128), jnp.bfloat16),
            pltpu.VMEM((512, 8), jnp.float32),
            pltpu.VMEM((72, 8, 128), jnp.float32),
        ),
        in_specs=[pl.BlockSpec(memory_space=pltpu.SMEM)] + [hbm] * 5,
        out_specs=(VMEM,) * 4,
        scratch_shapes=[
            pltpu.VMEM((3, 16), jnp.int32),
            pltpu.VMEM((1, 16), jnp.int32),
            pltpu.VMEM((3, 512), jnp.int32),
            pltpu.VMEM((6, 6, 2, 8), jnp.float32),
            pltpu.VMEM((8, 512), jnp.float32),
            pltpu.VMEM((128, 128), jnp.float32),
            pltpu.SemaphoreType.DMA((6,)),
            pltpu.SemaphoreType.DMA((4,)),
        ],
        compiler_params=pltpu.CompilerParams(vmem_limit_bytes=LIMIT),
        name="fetch",
    )(place, *(pltpu.with_memory_space_constraint(x, pltpu.HBM) for x in (coupling, coords, degeneracy, qpoints, eigvec)))


def pack_kernel(blocks, mine, out):
    @pl.loop(0, 8, unroll=2)
    def _(pair):
        for m in range(6):
            for half in range(2):
                a = blocks[m, 16 * half + pair]
                b = blocks[m, 16 * half + 8 + pair]
                at = pl.ds((m % 3 * 2 + half) * 32, 32)
                out[4 * pair + m // 3, at, :] = jnp.concatenate([a[:, :64], b[:, :64]], axis=1)
                out[4 * pair + 2 + m // 3, at, :] = jnp.concatenate([a[:, 64:], b[:, 64:]], axis=1)
        for u in range(4):
            out[4 * pair + u, DATA_ROWS:ROWS, :] = mine[...]


def pack(blocks, mine):
    return pl.pallas_call(
        pack_kernel,
        out_shape=pltpu.VMEM((32, ROWS, 128), jnp.bfloat16),
        in_specs=[VMEM] * 2,
        out_specs=VMEM,
        compiler_params=pltpu.CompilerParams(vmem_limit_bytes=LIMIT),
        name="pack",
    )(on_chip(blocks), on_chip(mine))


CHUNK = 128


def combine_kernel(received, points, out, lattice, *tables):
    shift = 4.0 * (lax.broadcasted_iota(jnp.int32, (1, 128), 1) & 1).astype(jnp.float32)
    for k in range(8):
        at = slice(k * 128, k * 128 + 128)
        rows = received[4 * k : 4 * k + 4, DATA_ROWS:ROWS, :].astype(jnp.float32)
        rows = rows[0] + rows[1] + rows[2] + rows[3]
        lattice[0:3, at] = rows[0:3]
        lattice[3:4, at] = 1.0 / rows[3:4]
    c1, c2, c3 = (math.cos(2.0 * math.pi * i / QGRID) for i in (1, 2, 3))
    low = lax.broadcasted_iota(jnp.int32, (CHUNK, 128), 1) < 64

    for c, table in enumerate(tables):
        for piece in range(CHUNK // 32):
            q = points[c * CHUNK + piece * 32 : c * CHUNK + piece * 32 + 32, :]
            q0, q1, q2 = (jnp.broadcast_to(q[:, d : d + 1], (32, 128)) for d in range(3))
            for k in range(8):
                at = slice(k * 128, k * 128 + 128)
                turns = q0 * lattice[0:1, at] + q1 * lattice[1:2, at] + (q2 * lattice[2:3, at] + shift)
                turns = turns.astype(jnp.int32)
                bit0, bit1, bit2, bit3 = ((turns & b) != 0 for b in (1, 2, 4, 8))
                cosine = jnp.where(bit1, jnp.where(bit0, c3, c2), jnp.where(bit0, c1, 1.0))
                sine = jnp.where(bit1, jnp.where(bit0, c1, c2), jnp.where(bit0, c3, 0.0))
                weight = jnp.broadcast_to(lattice[3:4, at], (32, 128))
                sine_weight = jnp.where(bit3, -weight, weight)
                cosine_weight = jnp.where(bit2, -sine_weight, sine_weight)
                first = jnp.where(bit2, sine, cosine) * cosine_weight
                second = jnp.where(bit2, cosine, sine) * sine_weight
                table[piece * 32 : piece * 32 + 32, at] = first.astype(jnp.bfloat16)
                table[CHUNK + piece * 32 : CHUNK + piece * 32 + 32, at] = second.astype(jnp.bfloat16)

        owners = slice(c * CHUNK // 8, (c + 1) * CHUNK // 8)
        for m in range(3):
            columns = jnp.concatenate(
                [
                    received[:, m * 64 : m * 64 + 32, :].reshape(1024, 128),
                    received[:, m * 64 + 32 : m * 64 + 64, :].reshape(1024, 128),
                ],
                axis=1,
            )
            product = jnp.dot(table[...], columns, preferred_element_type=jnp.float32)
            rows = slice(m * 8, m * 8 + 8)
            for half in range(2):
                real = product[:CHUNK, 128 * half : 128 * half + 128]
                imag = product[CHUNK:, 128 * half : 128 * half + 128]
                near = jnp.where(low, real, pltpu.roll(imag, 64, 1))
                far = jnp.where(low, pltpu.roll(real, 64, 1), imag)
                out[owners, 2 * half, rows, :] = near.reshape(CHUNK // 8, 8, 128).astype(jnp.bfloat16)
                out[owners, 2 * half + 1, rows, :] = far.reshape(CHUNK // 8, 8, 128).astype(jnp.bfloat16)


def combine(received, points):
    return pl.pallas_call(
        combine_kernel,
        out_shape=pltpu.VMEM((64, 4, 24, 128), jnp.bfloat16),
        in_specs=[VMEM] * 2,
        out_specs=VMEM,
        scratch_shapes=[pltpu.VMEM((8, 1024), jnp.float32)]
        + [pltpu.VMEM((2 * CHUNK, 1024), jnp.bfloat16)] * (512 // CHUNK),
        compiler_params=pltpu.CompilerParams(vmem_limit_bytes=LIMIT),
        name="combine",
    )(on_chip(received), on_chip(points))


def rotate_kernel(summed, factors, out, result, sem):
    low = lax.broadcasted_iota(jnp.int32, (8, 128), 1) < 64

    @pl.loop(0, 4)
    def _(e):
        def piece(h, k):
            rows = slice(k % 3 * 8, k % 3 * 8 + 8)
            return summed[h, 0, k // 3, e, rows, :].astype(jnp.float32) + summed[
                h, 1, k // 3, e, rows, :
            ].astype(jnp.float32)

        @pl.loop(0, 4, unroll=4)
        def _(step):
            blocks = (2 * step, 2 * step + 1)
            real, imag = {}, {}
            for i, block in enumerate(blocks):
                for k in range(6):
                    left, right = piece(2 * block, k), piece(2 * block + 1, k)
                    real[i, k] = jnp.where(low, left, pltpu.roll(right, 64, 1))
                    imag[i, k] = jnp.where(low, pltpu.roll(left, 64, 1), right)
            for n in range(6):
                totals = {}
                for k in range(6):
                    vec_real = factors[k * 6 + n]
                    vec_imag = factors[36 + k * 6 + n]
                    for i in range(2):
                        terms = (
                            real[i, k] * vec_real - imag[i, k] * vec_imag,
                            real[i, k] * vec_imag + imag[i, k] * vec_real,
                        )
                        for part in range(2):
                            totals[i, part] = totals[i, part] + terms[part] if k else terms[part]
                for i, block in enumerate(blocks):
                    for part in range(2):
                        at = e * 96 + n * 16 + block * 2 + part
                        result[pl.ds(at, 8, stride=384), :] = totals[i, part]

        for q in range(8):
            at = pl.ds(pl.multiple_of(q * 384 + e * 96, 32), 96)
            pltpu.make_async_copy(result.at[at], out.at[at], sem).start()

    pltpu.make_async_copy(result, out, sem).wait()


def rotate(summed, factors):
    return pl.pallas_call(
        rotate_kernel,
        out_shape=jax.ShapeDtypeStruct((3072, 128), jnp.float32),
        in_specs=[VMEM] * 2,
        out_specs=pl.BlockSpec(memory_space=pltpu.HBM),
        scratch_shapes=[pltpu.VMEM((3072, 128), jnp.float32), pltpu.SemaphoreType.DMA],
        compiler_params=pltpu.CompilerParams(vmem_limit_bytes=LIMIT),
        name="rotate",
    )(on_chip(summed), on_chip(factors))


def per_device(coupling, rp_coords, degeneracy, qpoints, eigvec):
    place = (lax.axis_index(PLANE) % 4).astype(jnp.int32).reshape(1)
    blocks, mine, points, factors = fetch(
        place,
        coupling.reshape(16, 2, 6, 4096).transpose(0, 2, 1, 3),
        rp_coords,
        degeneracy.reshape(1, 16),
        qpoints,
        eigvec.transpose(2, 3, 1, 0),
    )
    message = pack(blocks.reshape(6, 32, 32, 128), mine)
    received = lax.all_to_all(message, PLANE, 0, 0, tiled=True)
    partial = combine(received, points).reshape(256, 24, 128)
    summed = lax.all_to_all(partial, EVERY, 0, 0, tiled=True)
    result = rotate(summed.reshape(16, 2, 2, 4, 24, 128), factors)
    return result.reshape(8, 4, 6, 8, 2, 128).transpose(0, 1, 4, 2, 3, 5).reshape(8, 4, 2, 6, 1024)


def solution(mesh):
    rp = ("y", "x", "zh", "core")
    inner = Mesh(mesh.devices.reshape(4, 4, 2, 2, 4), EVERY)
    return jax.shard_map(
        per_device,
        mesh=inner,
        in_specs=(P(rp, "re", None, None, None), P(None, rp), P(rp), P(), P(rp, None, None, None)),
        out_specs=P(rp, None, None, None, "re"),
        check_vma=False,
    )
```

time: 104 us -> 95.5 us (0.918)
  blocking collectives: 0 us -> 86 us
  waiting for transfers between devices: 65.4 us -> 0 us
  starting transfers between devices: 20 us -> 0 us
  Pallas kernels: 16.2 us -> 9.21 us
  local copies, waits for them, and re-layouts: 1.71 us -> 0 us
    all_to_all x0 -> x2, blocking collectives: none -> 86 us  [the longest x1 54.2 us: per_device(): summed = lax.all_to_all(partial, EVERY, 0, 0, tiled=True)]
    all_to_all x2 -> x0, waiting for transfers between devices: 65.4 us -> none  [the longest x1 42.7 us: per_device(): summed = lax.all_to_all(partial, EVERY, 0, 0, tiled=True)]
    all_to_all x2 -> x0, starting transfers between devices: 20 us -> none  [the longest x1 11.3 us: per_device(): summed = lax.all_to_all(partial, EVERY, 0, 0, tiled=True)]
    pallas_call x1, Pallas kernels: 7.91 us -> 3.75 us  [combine(): pl.pallas_call(combine_kernel, out_shape=pltpu.VMEM((64, 4, 24, 128), jnp...]
    pallas_call x1, Pallas kernels: 2.67 us -> 0.68 us  [pack(): pl.pallas_call(pack_kernel, out_shape=pltpu.VMEM((32, ROWS, 128), jnp.bfl...]
  transfers between devices with their start and end apart: 2 -> 0, of which waited for: 2 -> 0; matrix products, arithmetic and copies ran while one was open for 2% -> 0% of each run, Pallas kernels for 0% -> 0%
where the time goes in v3:
time: 95.5 us; the launch traced here: 95.2 us
  blocking collectives  86 us (90%)
  Pallas kernels  9.21 us (10%)
    all_to_all x1, blocking collectives, per_device(): summed = lax.all_to_all(partial, EVERY, 0, 0, tiled=True)  54.2 us
    all_to_all x1, blocking collectives, per_device(): received = lax.all_to_all(message, PLANE, 0, 0, tiled=True)  31.7 us
    pallas_call x1, Pallas kernels, combine(): pl.pallas_call(combine_kernel, out_shape=pltpu.VMEM((64, 4, 24, 128), jnp...  3.75 us
    pallas_call x1, Pallas kernels, rotate(): pl.pallas_call(rotate_kernel, out_shape=jax.ShapeDtypeStruct((3072, 128),...  3.04 us

profile of v3, /device:TPU:1, one launch (start us, length us, event | category | flops | bytes accessed | tf_op | source)
XLA Modules:
  0.0 95.2 jit_solution(3856960155487792719)
XLA Ops:
  0.0 1.7 %fetch.1 = (bf16[6,32,16,2,128]{4,3,2,1,0:T(2,128)(2,1)S(1)}, bf16[8,128]{1,0:T(8,128)(2,1)S(1)}, f32[512,8]{1,0:T(8,128)S(1)}, f32[72,8,128]{2,1,0:T(8,128)S(1)}) custom-call(s32[1]{0:T(128)} %bitcast.place, bf16[16,6,2,4096]{3,2,1,0:T(2,128)(2,1)} %bitcast.17, s32[3,16]{1,0:T(4,128)} %coords.1, s32[1,16]{1,0:T(1,128)} %bitcast.19, s32[3,512]{1,0:T(4,128)} %qpoints.1, ...), custom_call_target="tpu_custom_call" | custom-call | tf_op jit(solution)/shard_map/fetch/pallas_call | solution.py:80
  1.7 0.7 pack.1
  2.4 31.7 %all_to_all.10.received = bf16[32,200,128]{2,1,0:T(8,128)(2,1)S(1)} all-to-all(bf16[32,200,128]{2,1,0:T(8,128)(2,1)S(1)} %pack.1), channel_id=1, replica_groups=mesh['y'=4,'x'=4,'zh'=2,'core'=2,'re'=4] {'y','x','core'}, dimensions={0} | all-to-all | bytes 3276800 | tf_op jit(solution)/shard_map/all_to_all | solution.py:263
  34.2 3.8 %combine.1 = bf16[64,4,24,128]{3,2,1,0:T(8,128)(2,1)S(1)} custom-call(bf16[32,200,128]{2,1,0:T(8,128)(2,1)S(1)} %all_to_all.10.received, f32[512,8]{1,0:T(8,128)S(1)} %get-tuple-element.11.points), custom_call_target="tpu_custom_call" | custom-call | tf_op jit(solution)/shard_map/combine/pallas_call | solution.py:184
  37.9 54.2 %all_to_all.11 = bf16[256,24,128]{2,1,0:T(8,128)(2,1)S(1)} all-to-all(bf16[256,24,128]{2,1,0:T(8,128)(2,1)S(1)} %bitcast.14), channel_id=1, replica_groups=mesh['y'=4,'x'=4,'zh'=2,'core'=2,'re'=4] {'y','x','zh','core','re'}, dimensions={0} | all-to-all | bytes 3145728 | tf_op jit(solution)/shard_map/all_to_all | solution.py:265
  92.2 3.0 %rotate.1 = f32[3072,128]{1,0:T(8,128)} custom-call(bf16[16,2,2,4,24,128]{5,4,3,2,1,0:T(8,128)(2,1)S(1)} %bitcast.15, f32[72,8,128]{2,1,0:T(8,128)S(1)} %get-tuple-element.12.factors), custom_call_target="tpu_custom_call" | custom-call | tf_op jit(solution)/shard_map/rotate/pallas_call | solution.py:241

commit v4 on v3

--- a/solution.py
+++ b/solution.py
@@ -28,20 +28,21 @@
     for copy in small:
         copy.start()
     for m in range(6):
-        @pl.loop(0, 32, unroll=8)
-        def _(b):
-            pltpu.make_async_copy(
-                coupling.at[:, m, :, pl.ds(pl.multiple_of(b * 128, 128), 128)],
-                blocks.at[m, b],
-                sems.at[m],
-            ).start()
+        @pl.loop(0, 4)
+        def _(group):
+            for i in range(8):
+                b = group * 8 + i
+                pltpu.make_async_copy(
+                    coupling.at[:, m, :, pl.ds(pl.multiple_of(b * 128, 128), 128)],
+                    blocks.at[m, b],
+                    sems.at[m],
+                ).start(priority=i % 2)
     for copy in small:
         copy.wait()
 
     lane = lax.broadcasted_iota(jnp.int32, (16, 128), 1)
     row = lax.broadcasted_iota(jnp.int32, (16, 128), 0)
-    spread = (lane == place[0] * 32 + 2 * row) | (lane == place[0] * 32 + 2 * row + 1)
-    spread = spread.astype(jnp.float32).astype(jnp.bfloat16)
+    spread = (lane == place[0] * 16 + row).astype(jnp.float32).astype(jnp.bfloat16)
     rows[...] = jnp.zeros_like(rows)
     for at, values in ((slice(0, 3), coords_in), (slice(3, 4), degeneracy_in)):
         rows[at, 0:128] = jnp.dot(
@@ -102,16 +103,27 @@
     )(place, *(pltpu.with_memory_space_constraint(x, pltpu.HBM) for x in (coupling, coords, degeneracy, qpoints, eigvec)))
 
 
-def pack_kernel(blocks, mine, out):
+SLOTS = 8
+
+
+def pack_kernel(blocks, mine, out, halves):
     @pl.loop(0, 8, unroll=2)
     def _(pair):
+        slot = 0
         for m in range(6):
             for half in range(2):
                 a = blocks[m, 16 * half + pair]
                 b = blocks[m, 16 * half + 8 + pair]
-                at = pl.ds((m % 3 * 2 + half) * 32, 32)
-                out[4 * pair + m // 3, at, :] = jnp.concatenate([a[:, :64], b[:, :64]], axis=1)
-                out[4 * pair + 2 + m // 3, at, :] = jnp.concatenate([a[:, 64:], b[:, 64:]], axis=1)
+                at = (m % 3 * 2 + half) * 32
+                for u, piece in (
+                    (4 * pair + m // 3, jnp.concatenate([a[:, :64], b[:, :64]], axis=1)),
+                    (4 * pair + 2 + m // 3, jnp.concatenate([a[:, 64:], b[:, 64:]], axis=1)),
+                ):
+                    halves[slot] = piece.astype(jnp.float32)
+                    for part in range(2):
+                        rows = slice(at + 16 * part, at + 16 * part + 16)
+                        out[u, rows, :] = halves[slot, pl.ds(part, 16, stride=2), :].astype(jnp.bfloat16)
+                    slot = (slot + 1) % SLOTS
         for u in range(4):
             out[4 * pair + u, DATA_ROWS:ROWS, :] = mine[...]
 
@@ -122,20 +134,20 @@
         out_shape=pltpu.VMEM((32, ROWS, 128), jnp.bfloat16),
         in_specs=[VMEM] * 2,
         out_specs=VMEM,
+        scratch_shapes=[pltpu.VMEM((SLOTS, 32, 128), jnp.float32)],
         compiler_params=pltpu.CompilerParams(vmem_limit_bytes=LIMIT),
         name="pack",
     )(on_chip(blocks), on_chip(mine))
 
 
-CHUNK = 128
+CHUNK = 256
 
 
 def combine_kernel(received, points, out, lattice, *tables):
-    shift = 4.0 * (lax.broadcasted_iota(jnp.int32, (1, 128), 1) & 1).astype(jnp.float32)
-    for k in range(8):
+    for k in range(4):
         at = slice(k * 128, k * 128 + 128)
-        rows = received[4 * k : 4 * k + 4, DATA_ROWS:ROWS, :].astype(jnp.float32)
-        rows = rows[0] + rows[1] + rows[2] + rows[3]
+        rows = received[8 * k : 8 * k + 8, DATA_ROWS:ROWS, :].astype(jnp.float32)
+        rows = ((rows[0] + rows[1]) + (rows[2] + rows[3])) + ((rows[4] + rows[5]) + (rows[6] + rows[7]))
         lattice[0:3, at] = rows[0:3]
         lattice[3:4, at] = 1.0 / rows[3:4]
     c1, c2, c3 = (math.cos(2.0 * math.pi * i / QGRID) for i in (1, 2, 3))
@@ -145,27 +157,38 @@
         for piece in range(CHUNK // 32):
             q = points[c * CHUNK + piece * 32 : c * CHUNK + piece * 32 + 32, :]
             q0, q1, q2 = (jnp.broadcast_to(q[:, d : d + 1], (32, 128)) for d in range(3))
-            for k in range(8):
+            upper = slice(piece * 32, piece * 32 + 32)
+            lower = slice(CHUNK + piece * 32, CHUNK + piece * 32 + 32)
+            for k in range(4):
                 at = slice(k * 128, k * 128 + 128)
-                turns = q0 * lattice[0:1, at] + q1 * lattice[1:2, at] + (q2 * lattice[2:3, at] + shift)
+                other = slice(512 + k * 128, 512 + k * 128 + 128)
+                turns = q0 * lattice[0:1, at] + q1 * lattice[1:2, at] + q2 * lattice[2:3, at]
                 turns = turns.astype(jnp.int32)
                 bit0, bit1, bit2, bit3 = ((turns & b) != 0 for b in (1, 2, 4, 8))
-                cosine = jnp.where(bit1, jnp.where(bit0, c3, c2), jnp.where(bit0, c1, 1.0))
-                sine = jnp.where(bit1, jnp.where(bit0, c1, c2), jnp.where(bit0, c3, 0.0))
+                near = jnp.where(bit1, jnp.where(bit0, c3, c2), jnp.where(bit0, c1, 1.0))
+                far = jnp.where(bit1, jnp.where(bit0, c1, c2), jnp.where(bit0, c3, 0.0))
                 weight = jnp.broadcast_to(lattice[3:4, at], (32, 128))
                 sine_weight = jnp.where(bit3, -weight, weight)
                 cosine_weight = jnp.where(bit2, -sine_weight, sine_weight)
-                first = jnp.where(bit2, sine, cosine) * cosine_weight
-                second = jnp.where(bit2, cosine, sine) * sine_weight
-                table[piece * 32 : piece * 32 + 32, at] = first.astype(jnp.bfloat16)
-                table[CHUNK + piece * 32 : CHUNK + piece * 32 + 32, at] = second.astype(jnp.bfloat16)
+                cosine = (jnp.where(bit2, far, near) * cosine_weight).astype(jnp.bfloat16)
+                sine = (jnp.where(bit2, near, far) * sine_weight).astype(jnp.bfloat16)
+                table[upper, at] = cosine
+                table[upper, other] = -sine
+                table[lower, at] = sine
+                table[lower, other] = cosine
 
         owners = slice(c * CHUNK // 8, (c + 1) * CHUNK // 8)
         for m in range(3):
             columns = jnp.concatenate(
                 [
-                    received[:, m * 64 : m * 64 + 32, :].reshape(1024, 128),
-                    received[:, m * 64 + 32 : m * 64 + 64, :].reshape(1024, 128),
+                    jnp.concatenate(
+                        [
+                            received[:, at : at + 16, :].reshape(512, 128)
+                            for at in (m * 64 + half * 32, m * 64 + half * 32 + 16)
+                        ],
+                        axis=0,
+                    )
+                    for half in range(2)
                 ],
                 axis=1,
             )
@@ -174,10 +197,10 @@
             for half in range(2):
                 real = product[:CHUNK, 128 * half : 128 * half + 128]
                 imag = product[CHUNK:, 128 * half : 128 * half + 128]
-                near = jnp.where(low, real, pltpu.roll(imag, 64, 1))
-                far = jnp.where(low, pltpu.roll(real, 64, 1), imag)
-                out[owners, 2 * half, rows, :] = near.reshape(CHUNK // 8, 8, 128).astype(jnp.bfloat16)
-                out[owners, 2 * half + 1, rows, :] = far.reshape(CHUNK // 8, 8, 128).astype(jnp.bfloat16)
+                first = jnp.where(low, real, pltpu.roll(imag, 64, 1))
+                second = jnp.where(low, pltpu.roll(real, 64, 1), imag)
+                out[owners, 2 * half, rows, :] = first.reshape(CHUNK // 8, 8, 128).astype(jnp.bfloat16)
+                out[owners, 2 * half + 1, rows, :] = second.reshape(CHUNK // 8, 8, 128).astype(jnp.bfloat16)
 
 
 def combine(received, points):
@@ -186,7 +209,7 @@
         out_shape=pltpu.VMEM((64, 4, 24, 128), jnp.bfloat16),
         in_specs=[VMEM] * 2,
         out_specs=VMEM,
-        scratch_shapes=[pltpu.VMEM((8, 1024), jnp.float32)]
+        scratch_shapes=[pltpu.VMEM((8, 512), jnp.float32)]
         + [pltpu.VMEM((2 * CHUNK, 1024), jnp.bfloat16)] * (512 // CHUNK),
         compiler_params=pltpu.CompilerParams(vmem_limit_bytes=LIMIT),
         name="combine",
@@ -250,7 +273,7 @@
 
 
 def per_device(coupling, rp_coords, degeneracy, qpoints, eigvec):
-    place = (lax.axis_index(PLANE) % 4).astype(jnp.int32).reshape(1)
+    place = (lax.axis_index(PLANE) % 8).astype(jnp.int32).reshape(1)
     blocks, mine, points, factors = fetch(
         place,
         coupling.reshape(16, 2, 6, 4096).transpose(0, 2, 1, 3),

time: 95.5 us -> 94.5 us (0.990)
  no operation moved by 1% of the time
where the time goes in v4:
time: 94.5 us; the launch traced here: 94.3 us
  blocking collectives  86 us (91%)
  Pallas kernels  8.29 us (9%)
    all_to_all x1, blocking collectives, per_device(): summed = lax.all_to_all(partial, EVERY, 0, 0, tiled=True)  54.2 us
    all_to_all x1, blocking collectives, per_device(): received = lax.all_to_all(message, PLANE, 0, 0, tiled=True)  31.7 us
    pallas_call x1, Pallas kernels, rotate(): pl.pallas_call(rotate_kernel, out_shape=jax.ShapeDtypeStruct((3072, 128),...  3.04 us
    pallas_call x1, Pallas kernels, combine(): pl.pallas_call(combine_kernel, out_shape=pltpu.VMEM((64, 4, 24, 128), jnp...  2.82 us

profile of v4, /device:TPU:1, one launch (start us, length us, event | category | flops | bytes accessed | tf_op | source)
XLA Modules:
  0.0 94.3 jit_solution(17492322103913257652)
XLA Ops:
  0.0 1.5 %fetch.1 = (bf16[6,32,16,2,128]{4,3,2,1,0:T(2,128)(2,1)S(1)}, bf16[8,128]{1,0:T(8,128)(2,1)S(1)}, f32[512,8]{1,0:T(8,128)S(1)}, f32[72,8,128]{2,1,0:T(8,128)S(1)}) custom-call(s32[1]{0:T(128)} %bitcast.place, bf16[16,6,2,4096]{3,2,1,0:T(2,128)(2,1)} %bitcast.17, s32[3,16]{1,0:T(4,128)} %coords.1, s32[1,16]{1,0:T(1,128)} %bitcast.19, s32[3,512]{1,0:T(4,128)} %qpoints.1, ...), custom_call_target="tpu_custom_call" | custom-call | tf_op jit(solution)/shard_map/fetch/pallas_call | solution.py:81
  1.6 0.9 pack.1
  2.4 31.7 %all_to_all.10.received = bf16[32,200,128]{2,1,0:T(8,128)(2,1)S(1)} all-to-all(bf16[32,200,128]{2,1,0:T(8,128)(2,1)S(1)} %pack.1), channel_id=1, replica_groups=mesh['y'=4,'x'=4,'zh'=2,'core'=2,'re'=4] {'y','x','core'}, dimensions={0} | all-to-all | bytes 3276800 | tf_op jit(solution)/shard_map/all_to_all | solution.py:286
  34.2 2.8 %combine.1 = bf16[64,4,24,128]{3,2,1,0:T(8,128)(2,1)S(1)} custom-call(bf16[32,200,128]{2,1,0:T(8,128)(2,1)S(1)} %all_to_all.10.received, f32[512,8]{1,0:T(8,128)S(1)} %get-tuple-element.11.points), custom_call_target="tpu_custom_call" | custom-call | tf_op jit(solution)/shard_map/combine/pallas_call | solution.py:207
  37.0 54.2 %all_to_all.11 = bf16[256,24,128]{2,1,0:T(8,128)(2,1)S(1)} all-to-all(bf16[256,24,128]{2,1,0:T(8,128)(2,1)S(1)} %bitcast.14), channel_id=1, replica_groups=mesh['y'=4,'x'=4,'zh'=2,'core'=2,'re'=4] {'y','x','zh','core','re'}, dimensions={0} | all-to-all | bytes 3145728 | tf_op jit(solution)/shard_map/all_to_all | solution.py:288
  91.3 3.0 %rotate.1 = f32[3072,128]{1,0:T(8,128)} custom-call(bf16[16,2,2,4,24,128]{5,4,3,2,1,0:T(8,128)(2,1)S(1)} %bitcast.15, f32[72,8,128]{2,1,0:T(8,128)S(1)} %get-tuple-element.12.factors), custom_call_target="tpu_custom_call" | custom-call | tf_op jit(solution)/shard_map/rotate/pallas_call | solution.py:264

commit v5 on v4

--- a/solution.py
+++ b/solution.py
@@ -10,13 +10,14 @@
 QGRID = 16
 PLANE = ("y", "x", "core")
 EVERY = ("y", "x", "zh", "core", "re")
+OWNERS = ("core", "y", "x", "zh", "re")
 DATA_ROWS = 192
 ROWS = 200
 
 
 def fetch_kernel(
     place, coupling, coords, degeneracy, qpoints, eigvec,
-    blocks, mine, points, factors,
+    blocks, mine, points, rotation,
     coords_in, degeneracy_in, qpoints_in, eigvec_in, rows, columns, sems, small_sems,
 ):
     small = [
@@ -61,8 +62,22 @@
                 i = part * 36 + k * 6 + n
                 columns[i : i + 1, 0:8] = eigvec_in[k, n, part : part + 1, :]
     turned = jnp.transpose(columns[...])
-    for i in range(72):
-        factors[i] = jnp.broadcast_to(turned[0:8, i : i + 1], (8, 128))
+    lane = lax.broadcasted_iota(jnp.int32, (8, 128), 1)
+    mode = lane // 8
+    mode = jnp.where(mode < 6, mode, mode - 6)
+    same_point = (lane & 7) == lax.broadcasted_iota(jnp.int32, (8, 128), 0)
+    for part in range(2):
+        for n in range(6):
+            factor = jnp.zeros((8, 128), jnp.float32)
+            for k in range(6):
+                i = part * 36 + k * 6 + n
+                factor = jnp.where(mode == k, jnp.broadcast_to(turned[0:8, i : i + 1], (8, 128)), factor)
+            factor = jnp.where(same_point, factor, 0.0)
+            for term in range(3):
+                rounded = factor.astype(jnp.bfloat16)
+                at = term * 96 + part * 48 + n * 8
+                rotation[at : at + 8, :] = rounded[:, 0:96]
+                factor = factor - rounded.astype(jnp.float32)
 
     for m in range(6):
         pltpu.make_async_copy(blocks.at[m], blocks.at[m], sems.at[m]).wait()
@@ -84,7 +99,7 @@
             pltpu.VMEM((6, 32, 16, 2, 128), jnp.bfloat16),
             pltpu.VMEM((8, 128), jnp.bfloat16),
             pltpu.VMEM((512, 8), jnp.float32),
-            pltpu.VMEM((72, 8, 128), jnp.float32),
+            pltpu.VMEM((288, 96), jnp.bfloat16),
         ),
         in_specs=[pl.BlockSpec(memory_space=pltpu.SMEM)] + [hbm] * 5,
         out_specs=(VMEM,) * 4,
@@ -177,7 +192,7 @@
                 table[lower, at] = sine
                 table[lower, other] = cosine
 
-        owners = slice(c * CHUNK // 8, (c + 1) * CHUNK // 8)
+        owners = slice(c * CHUNK // 16, (c + 1) * CHUNK // 16)
         for m in range(3):
             columns = jnp.concatenate(
                 [
@@ -199,14 +214,16 @@
                 imag = product[CHUNK:, 128 * half : 128 * half + 128]
                 first = jnp.where(low, real, pltpu.roll(imag, 64, 1))
                 second = jnp.where(low, pltpu.roll(real, 64, 1), imag)
-                out[owners, 2 * half, rows, :] = first.reshape(CHUNK // 8, 8, 128).astype(jnp.bfloat16)
-                out[owners, 2 * half + 1, rows, :] = second.reshape(CHUNK // 8, 8, 128).astype(jnp.bfloat16)
+                for quarter, values in ((2 * half, first), (2 * half + 1, second)):
+                    values = values.reshape(CHUNK // 16, 2, 8, 128).astype(jnp.bfloat16)
+                    for core in range(2):
+                        out[core, owners, quarter, rows, :] = values[:, core]
 
 
 def combine(received, points):
     return pl.pallas_call(
         combine_kernel,
-        out_shape=pltpu.VMEM((64, 4, 24, 128), jnp.bfloat16),
+        out_shape=pltpu.VMEM((2, 32, 4, 24, 128), jnp.bfloat16),
         in_specs=[VMEM] * 2,
         out_specs=VMEM,
         scratch_shapes=[pltpu.VMEM((8, 512), jnp.float32)]
@@ -216,51 +233,45 @@
     )(on_chip(received), on_chip(points))
 
 
-def rotate_kernel(summed, factors, out, result, sem):
+GROUP = 4
+
+
+def rotate_kernel(summed, rotation, out, result, sem):
     low = lax.broadcasted_iota(jnp.int32, (8, 128), 1) < 64
-
-    @pl.loop(0, 4)
-    def _(e):
-        def piece(h, k):
-            rows = slice(k % 3 * 8, k % 3 * 8 + 8)
-            return summed[h, 0, k // 3, e, rows, :].astype(jnp.float32) + summed[
-                h, 1, k // 3, e, rows, :
-            ].astype(jnp.float32)
-
-        @pl.loop(0, 4, unroll=4)
-        def _(step):
-            blocks = (2 * step, 2 * step + 1)
-            real, imag = {}, {}
-            for i, block in enumerate(blocks):
-                for k in range(6):
-                    left, right = piece(2 * block, k), piece(2 * block + 1, k)
-                    real[i, k] = jnp.where(low, left, pltpu.roll(right, 64, 1))
-                    imag[i, k] = jnp.where(low, pltpu.roll(left, 64, 1), right)
-            for n in range(6):
-                totals = {}
-                for k in range(6):
-                    vec_real = factors[k * 6 + n]
-                    vec_imag = factors[36 + k * 6 + n]
-                    for i in range(2):
-                        terms = (
-                            real[i, k] * vec_real - imag[i, k] * vec_imag,
-                            real[i, k] * vec_imag + imag[i, k] * vec_real,
-                        )
-                        for part in range(2):
-                            totals[i, part] = totals[i, part] + terms[part] if k else terms[part]
-                for i, block in enumerate(blocks):
-                    for part in range(2):
-                        at = e * 96 + n * 16 + block * 2 + part
-                        result[pl.ds(at, 8, stride=384), :] = totals[i, part]
-
+    sign = jnp.where(low, 1.0, -1.0)
+    for e in range(4):
+        for group in range(16 // GROUP):
+            values = jnp.concatenate(
+                [
+                    jnp.concatenate(
+                        [summed[core, group * GROUP + run, half, e] for half in range(2) for core in range(2)], axis=0
+                    )
+                    for run in range(GROUP)
+                ],
+                axis=1,
+            )
+            product = jnp.dot(rotation[...], values, preferred_element_type=jnp.float32)
+            product = product[0:96] + product[96:192] + product[192:288]
+            for pair in range(GROUP // 2):
+                left = slice(pair * 256, pair * 256 + 128)
+                right = slice(pair * 256 + 128, pair * 256 + 256)
+                for n in range(6):
+                    by_real, by_imag = slice(n * 8, n * 8 + 8), slice(48 + n * 8, 56 + n * 8)
+                    a, b = product[by_real, left], product[by_real, right]
+                    c, d = product[by_imag, left], product[by_imag, right]
+                    real = (jnp.where(low, a, d) - pltpu.roll(jnp.where(low, b, c), 64, 1)) * sign
+                    imag = jnp.where(low, c, b) + pltpu.roll(jnp.where(low, d, a), 64, 1)
+                    at = e * 96 + n * 16 + (group * GROUP // 2 + pair) * 2
+                    result[pl.ds(at, 8, stride=384), :] = real
+                    result[pl.ds(at + 1, 8, stride=384), :] = imag
         for q in range(8):
-            at = pl.ds(pl.multiple_of(q * 384 + e * 96, 32), 96)
+            at = pl.ds(q * 384 + e * 96, 96)
             pltpu.make_async_copy(result.at[at], out.at[at], sem).start()
 
     pltpu.make_async_copy(result, out, sem).wait()
 
 
-def rotate(summed, factors):
+def rotate(summed, rotation):
     return pl.pallas_call(
         rotate_kernel,
         out_shape=jax.ShapeDtypeStruct((3072, 128), jnp.float32),
@@ -269,12 +280,12 @@
         scratch_shapes=[pltpu.VMEM((3072, 128), jnp.float32), pltpu.SemaphoreType.DMA],
         compiler_params=pltpu.CompilerParams(vmem_limit_bytes=LIMIT),
         name="rotate",
-    )(on_chip(summed), on_chip(factors))
+    )(on_chip(summed), on_chip(rotation))
 
 
 def per_device(coupling, rp_coords, degeneracy, qpoints, eigvec):
     place = (lax.axis_index(PLANE) % 8).astype(jnp.int32).reshape(1)
-    blocks, mine, points, factors = fetch(
+    blocks, mine, points, rotation = fetch(
         place,
         coupling.reshape(16, 2, 6, 4096).transpose(0, 2, 1, 3),
         rp_coords,
@@ -285,8 +296,8 @@
     message = pack(blocks.reshape(6, 32, 32, 128), mine)
     received = lax.all_to_all(message, PLANE, 0, 0, tiled=True)
     partial = combine(received, points).reshape(256, 24, 128)
-    summed = lax.all_to_all(partial, EVERY, 0, 0, tiled=True)
-    result = rotate(summed.reshape(16, 2, 2, 4, 24, 128), factors)
+    summed = lax.all_to_all(partial, OWNERS, 0, 0, tiled=True)
+    result = rotate(summed.reshape(2, 16, 2, 4, 24, 128), rotation)
     return result.reshape(8, 4, 6, 8, 2, 128).transpose(0, 1, 4, 2, 3, 5).reshape(8, 4, 2, 6, 1024)
 
 

time: 94.5 us -> 93.5 us (0.989)
  no operation moved by 1% of the time
where the time goes in v5:
time: 93.5 us; the launch traced here: 93.3 us
  blocking collectives  85.4 us (91%)
  Pallas kernels  7.89 us (8%)
    all_to_all x1, blocking collectives, per_device(): summed = lax.all_to_all(partial, OWNERS, 0, 0, tiled=True)  53.6 us
    all_to_all x1, blocking collectives, per_device(): received = lax.all_to_all(message, PLANE, 0, 0, tiled=True)  31.7 us
    pallas_call x1, Pallas kernels, combine(): pl.pallas_call(combine_kernel, out_shape=pltpu.VMEM((2, 32, 4, 24, 128),...  2.82 us
    pallas_call x1, Pallas kernels, rotate(): pl.pallas_call(rotate_kernel, out_shape=jax.ShapeDtypeStruct((3072, 128),...  2.63 us

profile of v5, /device:TPU:1, one launch (start us, length us, event | category | flops | bytes accessed | tf_op | source)
XLA Modules:
  0.0 93.3 jit_solution(9481807183781744083)
XLA Ops:
  0.0 1.5 %fetch.1 = (bf16[6,32,16,2,128]{4,3,2,1,0:T(2,128)(2,1)S(1)}, bf16[8,128]{1,0:T(8,128)(2,1)S(1)}, f32[512,8]{1,0:T(8,128)S(1)}, bf16[288,96]{1,0:T(8,128)(2,1)S(1)}) custom-call(s32[1]{0:T(128)} %bitcast.place, bf16[16,6,2,4096]{3,2,1,0:T(2,128)(2,1)} %bitcast.17, s32[3,16]{1,0:T(4,128)} %coords.1, s32[1,16]{1,0:T(1,128)} %bitcast.19, s32[3,512]{1,0:T(4,128)} %qpoints.1, ...), custom_call_target="tpu_custom_call" | custom-call | tf_op jit(solution)/shard_map/fetch/pallas_call | solution.py:96
  1.6 0.9 pack.1
  2.4 31.7 %all_to_all.10.received = bf16[32,200,128]{2,1,0:T(8,128)(2,1)S(1)} all-to-all(bf16[32,200,128]{2,1,0:T(8,128)(2,1)S(1)} %pack.1), channel_id=1, replica_groups=mesh['y'=4,'x'=4,'zh'=2,'core'=2,'re'=4] {'y','x','core'}, dimensions={0} | all-to-all | bytes 3276800 | tf_op jit(solution)/shard_map/all_to_all | solution.py:297
  34.2 2.8 %combine.1 = bf16[2,32,4,24,128]{4,3,2,1,0:T(8,128)(2,1)S(1)} custom-call(bf16[32,200,128]{2,1,0:T(8,128)(2,1)S(1)} %all_to_all.10.received, f32[512,8]{1,0:T(8,128)S(1)} %get-tuple-element.11.points), custom_call_target="tpu_custom_call" | custom-call | tf_op jit(solution)/shard_map/combine/pallas_call | solution.py:224
  37.0 53.6 %all_to_all.11 = bf16[256,24,128]{2,1,0:T(8,128)(2,1)S(1)} all-to-all(bf16[256,24,128]{2,1,0:T(8,128)(2,1)S(1)} %bitcast.15), channel_id=1, replica_groups=mesh['y'=4,'x'=4,'zh'=2,'core'=2,'re'=4] {'core','y','x','zh','re'}, dimensions={0} | all-to-all | bytes 3145728 | tf_op jit(solution)/shard_map/all_to_all | solution.py:299
  90.7 2.6 %rotate.1 = f32[3072,128]{1,0:T(8,128)} custom-call(bf16[2,16,2,4,24,128]{5,4,3,2,1,0:T(8,128)(2,1)S(1)} %bitcast.14, bf16[288,96]{1,0:T(8,128)(2,1)S(1)} %get-tuple-element.12.rotation), custom_call_target="tpu_custom_call" | custom-call | tf_op jit(solution)/shard_map/rotate/pallas_call | solution.py:275

commit v6 on v5

--- a/solution.py
+++ b/solution.py
@@ -118,11 +118,11 @@
     )(place, *(pltpu.with_memory_space_constraint(x, pltpu.HBM) for x in (coupling, coords, degeneracy, qpoints, eigvec)))
 
 
-SLOTS = 8
+SLOTS = 24
 
 
 def pack_kernel(blocks, mine, out, halves):
-    @pl.loop(0, 8, unroll=2)
+    @pl.loop(0, 8, unroll=8)
     def _(pair):
         slot = 0
         for m in range(6):

time: 93.5 us -> 93.3 us (level)
  no operation moved by 1% of the time
where the time goes in v6:
time: 93.3 us; the launch traced here: 93.1 us
  blocking collectives  85.4 us (92%)
  Pallas kernels  7.68 us (8%)
    all_to_all x1, blocking collectives, per_device(): summed = lax.all_to_all(partial, OWNERS, 0, 0, tiled=True)  53.6 us
    all_to_all x1, blocking collectives, per_device(): received = lax.all_to_all(message, PLANE, 0, 0, tiled=True)  31.7 us
    pallas_call x1, Pallas kernels, combine(): pl.pallas_call(combine_kernel, out_shape=pltpu.VMEM((2, 32, 4, 24, 128),...  2.83 us
    pallas_call x1, Pallas kernels, rotate(): pl.pallas_call(rotate_kernel, out_shape=jax.ShapeDtypeStruct((3072, 128),...  2.63 us

profile of v6, /device:TPU:1, one launch (start us, length us, event | category | flops | bytes accessed | tf_op | source)
XLA Modules:
  0.0 93.1 jit_solution(14324398709571122194)
XLA Ops:
  0.0 1.5 %fetch.1 = (bf16[6,32,16,2,128]{4,3,2,1,0:T(2,128)(2,1)S(1)}, bf16[8,128]{1,0:T(8,128)(2,1)S(1)}, f32[512,8]{1,0:T(8,128)S(1)}, bf16[288,96]{1,0:T(8,128)(2,1)S(1)}) custom-call(s32[1]{0:T(128)} %bitcast.place, bf16[16,6,2,4096]{3,2,1,0:T(2,128)(2,1)} %bitcast.17, s32[3,16]{1,0:T(4,128)} %coords.1, s32[1,16]{1,0:T(1,128)} %bitcast.19, s32[3,512]{1,0:T(4,128)} %qpoints.1, ...), custom_call_target="tpu_custom_call" | custom-call | tf_op jit(solution)/shard_map/fetch/pallas_call | solution.py:96
  1.6 0.7 pack.1
  2.2 31.7 %all_to_all.10.received = bf16[32,200,128]{2,1,0:T(8,128)(2,1)S(1)} all-to-all(bf16[32,200,128]{2,1,0:T(8,128)(2,1)S(1)} %pack.1), channel_id=1, replica_groups=mesh['y'=4,'x'=4,'zh'=2,'core'=2,'re'=4] {'y','x','core'}, dimensions={0} | all-to-all | bytes 3276800 | tf_op jit(solution)/shard_map/all_to_all | solution.py:297
  34.0 2.8 %combine.1 = bf16[2,32,4,24,128]{4,3,2,1,0:T(8,128)(2,1)S(1)} custom-call(bf16[32,200,128]{2,1,0:T(8,128)(2,1)S(1)} %all_to_all.10.received, f32[512,8]{1,0:T(8,128)S(1)} %get-tuple-element.11.points), custom_call_target="tpu_custom_call" | custom-call | tf_op jit(solution)/shard_map/combine/pallas_call | solution.py:224
  36.8 53.6 %all_to_all.11 = bf16[256,24,128]{2,1,0:T(8,128)(2,1)S(1)} all-to-all(bf16[256,24,128]{2,1,0:T(8,128)(2,1)S(1)} %bitcast.15), channel_id=1, replica_groups=mesh['y'=4,'x'=4,'zh'=2,'core'=2,'re'=4] {'core','y','x','zh','re'}, dimensions={0} | all-to-all | bytes 3145728 | tf_op jit(solution)/shard_map/all_to_all | solution.py:299
  90.5 2.6 %rotate.1 = f32[3072,128]{1,0:T(8,128)} custom-call(bf16[2,16,2,4,24,128]{5,4,3,2,1,0:T(8,128)(2,1)S(1)} %bitcast.14, bf16[288,96]{1,0:T(8,128)(2,1)S(1)} %get-tuple-element.12.rotation), custom_call_target="tpu_custom_call" | custom-call | tf_op jit(solution)/shard_map/rotate/pallas_call | solution.py:275

commit v7 on v6

--- a/solution.py
+++ b/solution.py
@@ -73,7 +73,7 @@
                 i = part * 36 + k * 6 + n
                 factor = jnp.where(mode == k, jnp.broadcast_to(turned[0:8, i : i + 1], (8, 128)), factor)
             factor = jnp.where(same_point, factor, 0.0)
-            for term in range(3):
+            for term in range(2):
                 rounded = factor.astype(jnp.bfloat16)
                 at = term * 96 + part * 48 + n * 8
                 rotation[at : at + 8, :] = rounded[:, 0:96]
@@ -99,7 +99,7 @@
             pltpu.VMEM((6, 32, 16, 2, 128), jnp.bfloat16),
             pltpu.VMEM((8, 128), jnp.bfloat16),
             pltpu.VMEM((512, 8), jnp.float32),
-            pltpu.VMEM((288, 96), jnp.bfloat16),
+            pltpu.VMEM((192, 96), jnp.bfloat16),
         ),
         in_specs=[pl.BlockSpec(memory_space=pltpu.SMEM)] + [hbm] * 5,
         out_specs=(VMEM,) * 4,
@@ -251,7 +251,7 @@
                 axis=1,
             )
             product = jnp.dot(rotation[...], values, preferred_element_type=jnp.float32)
-            product = product[0:96] + product[96:192] + product[192:288]
+            product = product[0:96] + product[96:192]
             for pair in range(GROUP // 2):
                 left = slice(pair * 256, pair * 256 + 128)
                 right = slice(pair * 256 + 128, pair * 256 + 256)

time: 93.3 us -> 93.1 us (level)
  no operation moved by 1% of the time
where the time goes in v7:
time: 93.1 us; the launch traced here: 92.9 us
  blocking collectives  85.4 us (92%)
  Pallas kernels  7.45 us (8%)
    all_to_all x1, blocking collectives, per_device(): summed = lax.all_to_all(partial, OWNERS, 0, 0, tiled=True)  53.6 us
    all_to_all x1, blocking collectives, per_device(): received = lax.all_to_all(message, PLANE, 0, 0, tiled=True)  31.7 us
    pallas_call x1, Pallas kernels, combine(): pl.pallas_call(combine_kernel, out_shape=pltpu.VMEM((2, 32, 4, 24, 128),...  2.83 us
    pallas_call x1, Pallas kernels, rotate(): pl.pallas_call(rotate_kernel, out_shape=jax.ShapeDtypeStruct((3072, 128),...  2.4 us

profile of v7, /device:TPU:1, one launch (start us, length us, event | category | flops | bytes accessed | tf_op | source)
XLA Modules:
  0.0 92.9 jit_solution(16201249061294429464)
XLA Ops:
  0.0 1.5 %fetch.1 = (bf16[6,32,16,2,128]{4,3,2,1,0:T(2,128)(2,1)S(1)}, bf16[8,128]{1,0:T(8,128)(2,1)S(1)}, f32[512,8]{1,0:T(8,128)S(1)}, bf16[192,96]{1,0:T(8,128)(2,1)S(1)}) custom-call(s32[1]{0:T(128)} %bitcast.place, bf16[16,6,2,4096]{3,2,1,0:T(2,128)(2,1)} %bitcast.17, s32[3,16]{1,0:T(4,128)} %coords.1, s32[1,16]{1,0:T(1,128)} %bitcast.19, s32[3,512]{1,0:T(4,128)} %qpoints.1, ...), custom_call_target="tpu_custom_call" | custom-call | tf_op jit(solution)/shard_map/fetch/pallas_call | solution.py:96
  1.6 0.7 pack.1
  2.2 31.7 %all_to_all.10.received = bf16[32,200,128]{2,1,0:T(8,128)(2,1)S(1)} all-to-all(bf16[32,200,128]{2,1,0:T(8,128)(2,1)S(1)} %pack.1), channel_id=1, replica_groups=mesh['y'=4,'x'=4,'zh'=2,'core'=2,'re'=4] {'y','x','core'}, dimensions={0} | all-to-all | bytes 3276800 | tf_op jit(solution)/shard_map/all_to_all | solution.py:297
  34.0 2.8 %combine.1 = bf16[2,32,4,24,128]{4,3,2,1,0:T(8,128)(2,1)S(1)} custom-call(bf16[32,200,128]{2,1,0:T(8,128)(2,1)S(1)} %all_to_all.10.received, f32[512,8]{1,0:T(8,128)S(1)} %get-tuple-element.11.points), custom_call_target="tpu_custom_call" | custom-call | tf_op jit(solution)/shard_map/combine/pallas_call | solution.py:224
  36.8 53.6 %all_to_all.11 = bf16[256,24,128]{2,1,0:T(8,128)(2,1)S(1)} all-to-all(bf16[256,24,128]{2,1,0:T(8,128)(2,1)S(1)} %bitcast.15), channel_id=1, replica_groups=mesh['y'=4,'x'=4,'zh'=2,'core'=2,'re'=4] {'core','y','x','zh','re'}, dimensions={0} | all-to-all | bytes 3145728 | tf_op jit(solution)/shard_map/all_to_all | solution.py:299
  90.5 2.4 %rotate.1 = f32[3072,128]{1,0:T(8,128)} custom-call(bf16[2,16,2,4,24,128]{5,4,3,2,1,0:T(8,128)(2,1)S(1)} %bitcast.14, bf16[192,96]{1,0:T(8,128)(2,1)S(1)} %get-tuple-element.12.rotation), custom_call_target="tpu_custom_call" | custom-call | tf_op jit(solution)/shard_map/rotate/pallas_call | solution.py:275
